TPU v7x, 32 devices: a 4x4x1 block of a 4x4x8 slice. The times are simulated.
32 devices in a mesh: dp: 1 (over z), tp: 4 (over y), cp: 8 (over x, core).
Axes of the slice: x: 4, y: 4, z: 1, core: 2. Of those that a mesh axis runs over, the one named last changes fastest.
The devices are a block of a 4x4x8 slice.
Arguments:
- hidden: bfloat16 [6, 3072, 2304], P('dp', 'cp')
- cotangent: bfloat16 [6, 3072, 2304], P('dp', 'cp')
- positions: int32 [3072], P(('dp', 'cp'))
- w_q: bfloat16 [2304, 2048], P(None, 'tp')
- w_k: bfloat16 [2304, 1024], P(None, 'tp')
- w_v: bfloat16 [2304, 1024], P(None, 'tp')
- w_o: bfloat16 [2048, 2304], P('tp')
- w_pre: float32 [2304], replicated
- w_post: float32 [2304], replicated
- q_norm: float32 [256], replicated
- k_norm: float32 [256], replicated
Outputs:
- output 1: bfloat16 [6, 3072, 2304], P('dp', 'cp')
- output 2: bfloat16 [6, 3072, 2304], P('dp', 'cp')
- output 3: float32 [2304, 2048], P('dp', 'tp')
- output 4: float32 [2304, 1024], P('dp', 'tp')
- output 5: float32 [2304, 1024], P('dp', 'tp')
- output 6: float32 [2048, 2304], P(('dp', 'tp'))
- output 7: float32 [2304], P('dp')
- output 8: float32 [2304], P('dp')
- output 9: float32 [256], P('dp')
- output 10: float32 [256], P('dp')
All inputs are finite; a program needn't handle non-finite values.
Results may differ from a plain program's by a relative error of at most 0.02.
Values are sent between devices in bfloat16 or wider.
A program may use at most 768 MiB of HBM per device.

v0:
```python
import jax
import jax.numpy as jnp
from jax import lax
from jax.sharding import PartitionSpec as P

EPS = 1e-6
ROPE_BASE = 1000000.0
ROPE_SCALE = 8.0
NEG_BIG = -1e30


def rms_unit(values):
    inv_rms = lax.rsqrt(jnp.mean(values * values, axis=-1, keepdims=True) + EPS)
    return values * inv_rms, inv_rms


def rms_unit_back(d_unit, unit_vals, inv_rms):
    return inv_rms * (d_unit - unit_vals * jnp.mean(d_unit * unit_vals, axis=-1, keepdims=True))


def rope_tables(pos_loc, head_dim):
    half_dim = head_dim // 2
    inv_freq = 1.0 / (ROPE_SCALE * ROPE_BASE ** (jnp.arange(half_dim, dtype=jnp.float32) * (2.0 / head_dim)))
    angles = pos_loc.astype(jnp.float32)[:, None] * inv_freq[None, :]
    return jnp.cos(angles)[None, :, None, :], jnp.sin(angles)[None, :, None, :]


def rope_apply(values, cos_t, sin_t):
    half_dim = values.shape[-1] // 2
    lower_half = values[..., :half_dim]
    upper_half = values[..., half_dim:]
    return jnp.concatenate([lower_half * cos_t - upper_half * sin_t, upper_half * cos_t + lower_half * sin_t], axis=-1)


def rope_back(grads_in, cos_t, sin_t):
    half_dim = grads_in.shape[-1] // 2
    lower_half = grads_in[..., :half_dim]
    upper_half = grads_in[..., half_dim:]
    return jnp.concatenate([lower_half * cos_t + upper_half * sin_t, upper_half * cos_t - lower_half * sin_t], axis=-1)


def head_norm(raw_heads, norm_gain, cos_t, sin_t):
    unit_vals, inv_rms = rms_unit(raw_heads.astype(jnp.float32))
    final_heads = rope_apply(unit_vals * (1.0 + norm_gain), cos_t, sin_t).astype(jnp.bfloat16)
    return final_heads, unit_vals, inv_rms


def head_norm_back(d_final, norm_gain, unit_vals, inv_rms, cos_t, sin_t):
    d_scaled = rope_back(d_final, cos_t, sin_t)
    d_gain = jnp.sum(d_scaled * unit_vals, axis=(0, 1, 2))
    return rms_unit_back(d_scaled * (1.0 + norm_gain), unit_vals, inv_rms), d_gain


def attend_block(run_stats, q_fin, k_blk, v_blk, q_pos, k_pos, score_scale):
    run_max, run_sum, run_acc = run_stats
    scores = jnp.einsum('bqkgd,bskd->bkgqs', q_fin, k_blk, preferred_element_type=jnp.float32) * score_scale
    allowed = k_pos[None, :] <= q_pos[:, None]
    new_max = jnp.maximum(run_max, jnp.max(jnp.where(allowed, scores, NEG_BIG), axis=-1))
    attn_prob = jnp.where(allowed, jnp.exp(scores - new_max[..., None]), 0.0)
    factor = jnp.exp(run_max - new_max)
    new_sum = run_sum * factor + jnp.sum(attn_prob, axis=-1)
    new_acc = run_acc * factor[..., None] + jnp.einsum('bkgqs,bskd->bkgqd', attn_prob.astype(jnp.bfloat16), v_blk, preferred_element_type=jnp.float32)
    return new_max, new_sum, new_acc


def grad_block(q_fin, d_out, log_norm, row_delta, q_pos, k_blk, v_blk, k_pos, score_scale):
    scores = jnp.einsum('bqkgd,bskd->bkgqs', q_fin, k_blk, preferred_element_type=jnp.float32) * score_scale
    allowed = k_pos[None, :] <= q_pos[:, None]
    attn_prob = jnp.where(allowed, jnp.exp(scores - log_norm[..., None]), 0.0)
    grad_v = jnp.einsum('bkgqs,bkgqd->bskd', attn_prob.astype(jnp.bfloat16), d_out, preferred_element_type=jnp.float32)
    d_prob = jnp.einsum('bkgqd,bskd->bkgqs', d_out, v_blk, preferred_element_type=jnp.float32)
    d_score = (attn_prob * (d_prob - row_delta[..., None]) * score_scale).astype(jnp.bfloat16)
    grad_q = jnp.einsum('bkgqs,bskd->bqkgd', d_score, k_blk, preferred_element_type=jnp.float32)
    grad_k = jnp.einsum('bkgqs,bqkgd->bskd', d_score, q_fin, preferred_element_type=jnp.float32)
    return grad_q, grad_k, grad_v


def solution(mesh):
    n_cp = mesh.shape['cp']
    next_hop = [(dev_idx, (dev_idx + 1) % n_cp) for dev_idx in range(n_cp)]

    def per_device(hidden, cotangent, pos_loc, w_q, w_k, w_v, w_o, w_pre, w_post, q_norm, k_norm):
        head_dim = q_norm.shape[0]
        n_batch, seq_loc, model_dim = hidden.shape
        q_heads = w_q.shape[1] // head_dim
        kv_heads = w_k.shape[1] // head_dim
        groups = q_heads // kv_heads
        score_scale = head_dim ** -0.5
        cos_t, sin_t = rope_tables(pos_loc, head_dim)

        x_f32 = hidden.astype(jnp.float32)
        x_unit, x_inv = rms_unit(x_f32)
        normed = (x_unit * (1.0 + w_pre)).astype(jnp.bfloat16)
        q_raw = jnp.einsum('bsd,dh->bsh', normed, w_q, preferred_element_type=jnp.float32).astype(jnp.bfloat16).reshape(n_batch, seq_loc, q_heads, head_dim)
        k_raw = jnp.einsum('bsd,dh->bsh', normed, w_k, preferred_element_type=jnp.float32).astype(jnp.bfloat16).reshape(n_batch, seq_loc, kv_heads, head_dim)
        v_loc = jnp.einsum('bsd,dh->bsh', normed, w_v, preferred_element_type=jnp.float32).astype(jnp.bfloat16).reshape(n_batch, seq_loc, kv_heads, head_dim)
        q_fin, q_unit, q_inv = head_norm(q_raw, q_norm, cos_t, sin_t)
        k_fin, k_unit, k_inv = head_norm(k_raw, k_norm, cos_t, sin_t)
        q_fin = q_fin.reshape(n_batch, seq_loc, kv_heads, groups, head_dim)

        stat_shape = (n_batch, kv_heads, groups, seq_loc)
        init_stats = (jnp.full(stat_shape, NEG_BIG, jnp.float32), jnp.zeros(stat_shape, jnp.float32), jnp.zeros(stat_shape + (head_dim,), jnp.float32))
        run_stats = attend_block(init_stats, q_fin, k_fin, v_loc, pos_loc, pos_loc, score_scale)

        def fwd_step(step_idx, loop_state):
            k_blk, v_blk, k_pos, carried = loop_state
            k_blk, v_blk, k_pos = lax.ppermute((k_blk, v_blk, k_pos), 'cp', next_hop)
            return k_blk, v_blk, k_pos, attend_block(carried, q_fin, k_blk, v_blk, pos_loc, k_pos, score_scale)

        final_state = lax.fori_loop(0, n_cp - 1, fwd_step, (k_fin, v_loc, pos_loc, run_stats))
        run_max, run_sum, run_acc = final_state[3]
        out_f32 = run_acc / run_sum[..., None]
        log_norm = run_max + jnp.log(run_sum)
        out_bf = out_f32.astype(jnp.bfloat16)
        wo_split = w_o.reshape(kv_heads, groups, head_dim, model_dim)
        attn = lax.psum(jnp.einsum('bkgqd,kgdm->bqm', out_bf, wo_split, preferred_element_type=jnp.float32), 'tp')
        attn_unit, attn_inv = rms_unit(attn)
        output = (x_f32 + attn_unit * (1.0 + w_post)).astype(jnp.bfloat16)

        grad_y = cotangent.astype(jnp.float32)
        d_post = lax.psum(jnp.sum(grad_y * attn_unit, axis=(0, 1)), 'cp')
        d_attn = rms_unit_back(grad_y * (1.0 + w_post), attn_unit, attn_inv).astype(jnp.bfloat16)
        d_wo = lax.psum(jnp.einsum('bkgqd,bqm->kgdm', out_bf, d_attn, preferred_element_type=jnp.float32), 'cp').reshape(q_heads * head_dim, model_dim)
        d_out = jnp.einsum('bqm,kgdm->bkgqd', d_attn, wo_split, preferred_element_type=jnp.float32)
        row_delta = jnp.sum(d_out * out_f32, axis=-1)
        d_out_bf = d_out.astype(jnp.bfloat16)

        dq_first, dk_first, dv_first = grad_block(q_fin, d_out_bf, log_norm, row_delta, pos_loc, k_fin, v_loc, pos_loc, score_scale)

        def bwd_step(step_idx, loop_state):
            k_blk, v_blk, k_pos, dk_run, dv_run, dq_run = loop_state
            k_blk, v_blk, k_pos, dk_run, dv_run = lax.ppermute((k_blk, v_blk, k_pos, dk_run, dv_run), 'cp', next_hop)
            grad_q, grad_k, grad_v = grad_block(q_fin, d_out_bf, log_norm, row_delta, pos_loc, k_blk, v_blk, k_pos, score_scale)
            return k_blk, v_blk, k_pos, dk_run + grad_k, dv_run + grad_v, dq_run + grad_q

        back_state = lax.fori_loop(0, n_cp - 1, bwd_step, (k_fin, v_loc, pos_loc, dk_first, dv_first, dq_first))
        dk_home, dv_home = lax.ppermute((back_state[3], back_state[4]), 'cp', next_hop)
        dq_all = back_state[5].reshape(n_batch, seq_loc, q_heads, head_dim)

        dq_raw, dq_gain = head_norm_back(dq_all, q_norm, q_unit, q_inv, cos_t, sin_t)
        dk_raw, dk_gain = head_norm_back(dk_home, k_norm, k_unit, k_inv, cos_t, sin_t)
        dq_bf = dq_raw.reshape(n_batch, seq_loc, q_heads * head_dim).astype(jnp.bfloat16)
        dk_bf = dk_raw.reshape(n_batch, seq_loc, kv_heads * head_dim).astype(jnp.bfloat16)
        dv_bf = dv_home.reshape(n_batch, seq_loc, kv_heads * head_dim).astype(jnp.bfloat16)
        d_wq = lax.psum(jnp.einsum('bsd,bsh->dh', normed, dq_bf, preferred_element_type=jnp.float32), 'cp')
        d_wk = lax.psum(jnp.einsum('bsd,bsh->dh', normed, dk_bf, preferred_element_type=jnp.float32), 'cp')
        d_wv = lax.psum(jnp.einsum('bsd,bsh->dh', normed, dv_bf, preferred_element_type=jnp.float32), 'cp')
        d_normed = lax.psum(jnp.einsum('bsh,dh->bsd', dq_bf, w_q, preferred_element_type=jnp.float32) + jnp.einsum('bsh,dh->bsd', dk_bf, w_k, preferred_element_type=jnp.float32) + jnp.einsum('bsh,dh->bsd', dv_bf, w_v, preferred_element_type=jnp.float32), 'tp')
        d_qnorm = lax.psum(dq_gain, ('tp', 'cp'))
        d_knorm = lax.psum(dk_gain, ('tp', 'cp'))
        d_pre = lax.psum(jnp.sum(d_normed * x_unit, axis=(0, 1)), 'cp')
        d_hidden = (grad_y + rms_unit_back(d_normed * (1.0 + w_pre), x_unit, x_inv)).astype(jnp.bfloat16)
        return output, d_hidden, d_wq, d_wk, d_wv, d_wo, d_pre, d_post, d_qnorm, d_knorm

    specs_in = (P('dp', 'cp', None), P('dp', 'cp', None), P(('dp', 'cp')), P(None, 'tp'), P(None, 'tp'), P(None, 'tp'), P('tp', None), P(None), P(None), P(None), P(None))
    specs_out = (P('dp', 'cp', None), P('dp', 'cp', None), P('dp', 'tp'), P('dp', 'tp'), P('dp', 'tp'), P(('dp', 'tp'), None), P('dp'), P('dp'), P('dp'), P('dp'))
    return jax.shard_map(per_device, mesh=mesh, in_specs=specs_in, out_specs=specs_out, check_vma=False)
```

profile of v0, /device:TPU:97, one launch (start us, length us, event | category | flops | bytes accessed | tf_op | source)
XLA Modules:
  0.0 2022.2 jit_solution(15174075036639698867)
XLA Ops:
  21.6 7.8 convolution_convert_fusion
  31.4 7.7 fusion.108
  47.1 10.7 convert_convert_fusion
  57.9 6.8 reshape.423
  88.3 242.0 %while.40 = (s32[]{:T(128)}, bf16[6,384,1,256]{3,1,0,2:T(8,128)(2,1)}, bf16[6,384,1,256]{3,1,0,2:T(8,128)(2,1)}, s32[384]{0:T(512)S(1)}, f32[6,1,2,384]{3,2,0,1:...) while((s32[]{:T(128)}, ...), condition=%wide.region_8.9_spmd, body=%wide.region_5.8_spmd.sunk | while | flops 1833924096 | bytes 83693952 | solution.py:110
  92.7 11.4 collective-permute-done.2
  127.2 11.4 collective-permute-done.2
  161.8 11.4 collective-permute-done.2
  196.3 11.4 collective-permute-done.2
  230.9 11.4 collective-permute-done.2
  265.4 11.4 collective-permute-done.2
  300.0 11.4 collective-permute-done.2
  336.4 12.3 convolution_bitcast_fusion
  355.4 7.3 mul.456
  362.8 357.3 %all-reduce.7.cloned.1.call-done = f32[6,384,2304]{2,1,0:T(8,128)} async-done(((f32[6,384,2304]{2,1,0:T(8,128)}), f32[6,384,2304]{2,1,0:T(8,128)}) %all-reduce.7.cloned.1.call-update) | async-done | bytes 21233680 | tf_op jit(solution)/shard_map/psum | solution.py:116
  720.0 9.1 multiply_reduce_fusion
  733.2 10.1 fusion.68
  743.3 19.7 fusion.69
  763.0 9.8 fusion.80
  801.4 589.0 %while.41 = (s32[]{:T(128)}, bf16[6,384,1,256]{3,1,0,2:T(8,128)(2,1)}, bf16[6,384,1,256]{3,1,0,2:T(8,128)(2,1)}, s32[384]{0:T(512)S(1)}, f32[6,384,1,256]{3,1,0,...) while((s32[]{:T(128)}, ...), condition=%wide.region_14.15_spmd, body=%wide.region_13.14_spmd.sunk | while | flops 4551819264 | bytes 140003888 | solution.py:136
  807.5 48.2 %collective-permute-done.5 = s32[384]{0:T(512)S(1)} collective-permute-done((s32[384]{0:T(512)S(1)}, s32[384]{0:T(512)S(1)}, u32[]{:S(2)}, u32[]{:S(2)}) %collective-permute-start.5) | collective-permute-done | bytes 1568 | tf_op jit(solution)/shard_map/while/body/eval_jaxpr/ppermute | solution.py:132
  872.7 8.3 collective-permute-done.6
  891.7 48.2 %collective-permute-done.5 = s32[384]{0:T(512)S(1)} collective-permute-done((s32[384]{0:T(512)S(1)}, s32[384]{0:T(512)S(1)}, u32[]{:S(2)}, u32[]{:S(2)}) %collective-permute-start.5) | collective-permute-done | bytes 1568 | tf_op jit(solution)/shard_map/while/body/eval_jaxpr/ppermute | solution.py:132
  956.9 8.3 collective-permute-done.6
  975.9 48.2 %collective-permute-done.5 = s32[384]{0:T(512)S(1)} collective-permute-done((s32[384]{0:T(512)S(1)}, s32[384]{0:T(512)S(1)}, u32[]{:S(2)}, u32[]{:S(2)}) %collective-permute-start.5) | collective-permute-done | bytes 1568 | tf_op jit(solution)/shard_map/while/body/eval_jaxpr/ppermute | solution.py:132
  1041.1 8.3 collective-permute-done.6
  1060.2 48.2 %collective-permute-done.5 = s32[384]{0:T(512)S(1)} collective-permute-done((s32[384]{0:T(512)S(1)}, s32[384]{0:T(512)S(1)}, u32[]{:S(2)}, u32[]{:S(2)}) %collective-permute-start.5) | collective-permute-done | bytes 1568 | tf_op jit(solution)/shard_map/while/body/eval_jaxpr/ppermute | solution.py:132
  1125.3 8.3 collective-permute-done.6
  1144.4 48.2 %collective-permute-done.5 = s32[384]{0:T(512)S(1)} collective-permute-done((s32[384]{0:T(512)S(1)}, s32[384]{0:T(512)S(1)}, u32[]{:S(2)}, u32[]{:S(2)}) %collective-permute-start.5) | collective-permute-done | bytes 1568 | tf_op jit(solution)/shard_map/while/body/eval_jaxpr/ppermute | solution.py:132
  1209.5 8.3 collective-permute-done.6
  1228.6 48.2 %collective-permute-done.5 = s32[384]{0:T(512)S(1)} collective-permute-done((s32[384]{0:T(512)S(1)}, s32[384]{0:T(512)S(1)}, u32[]{:S(2)}, u32[]{:S(2)}) %collective-permute-start.5) | collective-permute-done | bytes 1568 | tf_op jit(solution)/shard_map/while/body/eval_jaxpr/ppermute | solution.py:132
  1293.8 8.3 collective-permute-done.6
  1312.8 48.2 %collective-permute-done.5 = s32[384]{0:T(512)S(1)} collective-permute-done((s32[384]{0:T(512)S(1)}, s32[384]{0:T(512)S(1)}, u32[]{:S(2)}, u32[]{:S(2)}) %collective-permute-start.5) | collective-permute-done | bytes 1568 | tf_op jit(solution)/shard_map/while/body/eval_jaxpr/ppermute | solution.py:132
  1378.0 8.3 collective-permute-done.6
  1415.6 7.2 mul.477
  1422.8 7.3 multiply_reduce_fusion.1
  1431.6 10.1 fusion.114
  1445.5 8.7 fusion.135
  1454.2 22.9 %add_add_fusion = f32[6,384,2304]{2,1,0:T(8,128)} fusion(f32[6,384,2304]{2,1,0:T(8,128)} %fusion.114, f32[6,384,2304]{2,1,0:T(8,128)} %fusion.135, bf16[2304,256]{1,0:T(8,128)(2,1)S(1)} %copy-done.41, bf16[6,384,1,256]{3,1,0,2:T(8,128)(2,1)} %collective-permute-done.9), kind=kOutput, calls=%fused_computation.78 | convolution fusion | flops 2728525824 | bytes 66060288 | tf_op jit(solution)/shard_map/bsh,dh->bsd/dot_general | solution.py:148
  1477.3 12.1 fusion.111
  1489.4 10.2 convolution_bitcast_fusion.1
  1499.6 7.1 convolution_bitcast_fusion.2
  1513.3 54.2 %all-reduce = (f32[256]{0:T(256)}, f32[256]{0:T(256)}) all-reduce(f32[256]{0:T(256)S(1)} %reduce_sum.164, f32[256]{0:T(256)S(1)} %copy-done.67), channel_id=1, replica_groups=mesh['dp'=1,'tp'=4,'cp'=8] {'tp','cp'}, use_global_device_ids=true, to_apply=%region_29.30 | all-reduce | flops 512 | bytes 4096 | tf_op jit(solution)/shard_map/psum | solution.py:149
  1567.5 279.7 %all-reduce.9.cloned.1.call-done = f32[6,384,2304]{2,1,0:T(8,128)} async-done(((f32[6,384,2304]{2,1,0:T(8,128)}), f32[6,384,2304]{2,1,0:T(8,128)}) %all-reduce.9.cloned.1.call-update) | async-done | bytes 21233680 | tf_op jit(solution)/shard_map/psum | solution.py:148
  1847.2 12.5 fusion.64
  1859.7 24.0 %all-reduce.1 = (f32[2304]{0:T(1024)}, f32[2304]{0:T(1024)}) all-reduce(f32[2304]{0:T(1024)S(1)} %get-tuple-element.236, f32[2304]{0:T(1024)S(1)} %copy-done.58), channel_id=1, replica_groups=mesh['dp'=1,'tp'=4,'cp'=8] {'cp'}, use_global_device_ids=true, to_apply=%region_24.25 | all-reduce | flops 4608 | bytes 36864 | tf_op jit(solution)/shard_map/psum | solution.py:151
  1883.7 19.1 fusion.67
  1902.8 101.3 %all-reduce.11.cloned.1.call-done = (f32[2304,512]{1,0:T(8,128)}, f32[2304,256]{1,0:T(8,128)}, f32[2304,256]{1,0:T(8,128)}, f32[512,2304]{1,0:T(8,128)}) async-done(((f32[2304,512]{1,0:T(8,128)}, f32[2304,256]{1,0:T(8,128)}, f32[2304,256]{1,0:T(8,128)}, f32[512,2304]{1,0:T(8,128)}), (f32[2304,512]{1,0:T(8,128)}, f32[2304,256]{1,0:T(8,128)}, f32[2304,256]{1,0:T(8,128)}, ...) | async-done | bytes 14155792 | tf_op jit(solution)/shard_map/psum | solution.py:145
  (653 shorter events, 495.9 us)
Async XLA Ops:
  7.2 712.8 %all-reduce.7.cloned.1.call-start = ((), (), s32[]{:S(2)}) async-start(), calls=%async_computation | async-start | bytes 42467328 | tf_op jit(solution)/shard_map/psum | solution.py:116
  88.3 16.0 collective-permute-start
  91.0 25.7 %collective-permute-start.1 = (bf16[6,384,1,256]{3,1,0,2:T(8,128)(2,1)}, bf16[6,384,1,256]{3,1,0,2:T(8,128)(2,1)S(1)}, u32[]{:S(2)}, u32[]{:S(2)}) collective-permute-start(bf16[6,384,1,256]{3,1,0,2:T(8,128)(2,1)} %get-tuple-element.469), channel_id=1, source_target_pairs={{0,1},{1,2},{2,3},{3,4},{4,5},{5,6},{6,7},{7,0},{8,9},{9,10},{10,1... | collective-permute-start | bytes 3538952 | tf_op jit(solution)/shard_map/while/body/eval_jaxpr/ppermute | solution.py:107
  125.5 25.8 %collective-permute-start.1 = (bf16[6,384,1,256]{3,1,0,2:T(8,128)(2,1)}, bf16[6,384,1,256]{3,1,0,2:T(8,128)(2,1)S(1)}, u32[]{:S(2)}, u32[]{:S(2)}) collective-permute-start(bf16[6,384,1,256]{3,1,0,2:T(8,128)(2,1)} %get-tuple-element.469), channel_id=1, source_target_pairs={{0,1},{1,2},{2,3},{3,4},{4,5},{5,6},{6,7},{7,0},{8,9},{9,10},{10,1... | collective-permute-start | bytes 3538952 | tf_op jit(solution)/shard_map/while/body/eval_jaxpr/ppermute | solution.py:107
  160.1 25.8 %collective-permute-start.1 = (bf16[6,384,1,256]{3,1,0,2:T(8,128)(2,1)}, bf16[6,384,1,256]{3,1,0,2:T(8,128)(2,1)S(1)}, u32[]{:S(2)}, u32[]{:S(2)}) collective-permute-start(bf16[6,384,1,256]{3,1,0,2:T(8,128)(2,1)} %get-tuple-element.469), channel_id=1, source_target_pairs={{0,1},{1,2},{2,3},{3,4},{4,5},{5,6},{6,7},{7,0},{8,9},{9,10},{10,1... | collective-permute-start | bytes 3538952 | tf_op jit(solution)/shard_map/while/body/eval_jaxpr/ppermute | solution.py:107
  194.6 25.8 %collective-permute-start.1 = (bf16[6,384,1,256]{3,1,0,2:T(8,128)(2,1)}, bf16[6,384,1,256]{3,1,0,2:T(8,128)(2,1)S(1)}, u32[]{:S(2)}, u32[]{:S(2)}) collective-permute-start(bf16[6,384,1,256]{3,1,0,2:T(8,128)(2,1)} %get-tuple-element.469), channel_id=1, source_target_pairs={{0,1},{1,2},{2,3},{3,4},{4,5},{5,6},{6,7},{7,0},{8,9},{9,10},{10,1... | collective-permute-start | bytes 3538952 | tf_op jit(solution)/shard_map/while/body/eval_jaxpr/ppermute | solution.py:107
  229.1 25.8 %collective-permute-start.1 = (bf16[6,384,1,256]{3,1,0,2:T(8,128)(2,1)}, bf16[6,384,1,256]{3,1,0,2:T(8,128)(2,1)S(1)}, u32[]{:S(2)}, u32[]{:S(2)}) collective-permute-start(bf16[6,384,1,256]{3,1,0,2:T(8,128)(2,1)} %get-tuple-element.469), channel_id=1, source_target_pairs={{0,1},{1,2},{2,3},{3,4},{4,5},{5,6},{6,7},{7,0},{8,9},{9,10},{10,1... | collective-permute-start | bytes 3538952 | tf_op jit(solution)/shard_map/while/body/eval_jaxpr/ppermute | solution.py:107
  263.7 25.8 %collective-permute-start.1 = (bf16[6,384,1,256]{3,1,0,2:T(8,128)(2,1)}, bf16[6,384,1,256]{3,1,0,2:T(8,128)(2,1)S(1)}, u32[]{:S(2)}, u32[]{:S(2)}) collective-permute-start(bf16[6,384,1,256]{3,1,0,2:T(8,128)(2,1)} %get-tuple-element.469), channel_id=1, source_target_pairs={{0,1},{1,2},{2,3},{3,4},{4,5},{5,6},{6,7},{7,0},{8,9},{9,10},{10,1... | collective-permute-start | bytes 3538952 | tf_op jit(solution)/shard_map/while/body/eval_jaxpr/ppermute | solution.py:107
  298.2 25.8 %collective-permute-start.1 = (bf16[6,384,1,256]{3,1,0,2:T(8,128)(2,1)}, bf16[6,384,1,256]{3,1,0,2:T(8,128)(2,1)S(1)}, u32[]{:S(2)}, u32[]{:S(2)}) collective-permute-start(bf16[6,384,1,256]{3,1,0,2:T(8,128)(2,1)} %get-tuple-element.469), channel_id=1, source_target_pairs={{0,1},{1,2},{2,3},{3,4},{4,5},{5,6},{6,7},{7,0},{8,9},{9,10},{10,1... | collective-permute-start | bytes 3538952 | tf_op jit(solution)/shard_map/while/body/eval_jaxpr/ppermute | solution.py:107
  348.8 1498.4 %all-reduce.9.cloned.1.call-start = ((), (), s32[]{:S(2)}) async-start(), calls=%async_computation.1 | async-start | bytes 42467328 | tf_op jit(solution)/shard_map/psum | solution.py:148
  802.6 53.2 %collective-permute-start.3 = (bf16[6,384,1,256]{3,1,0,2:T(8,128)(2,1)}, bf16[6,384,1,256]{3,1,0,2:T(8,128)(2,1)S(1)}, u32[]{:S(2)}, u32[]{:S(2)}) collective-permute-start(bf16[6,384,1,256]{3,1,0,2:T(8,128)(2,1)} %get-tuple-element.501), channel_id=1, source_target_pairs={{0,1},{1,2},{2,3},{3,4},{4,5},{5,6},{6,7},{7,0},{8,9},{9,10},{10,1... | collective-permute-start | bytes 3538952 | tf_op jit(solution)/shard_map/while/body/eval_jaxpr/ppermute | solution.py:132
  804.6 53.4 %collective-permute-start.4 = (bf16[6,384,1,256]{3,1,0,2:T(8,128)(2,1)}, bf16[6,384,1,256]{3,1,0,2:T(8,128)(2,1)}, u32[]{:S(2)}, u32[]{:S(2)}) collective-permute-start(bf16[6,384,1,256]{3,1,0,2:T(8,128)(2,1)} %get-tuple-element.502), channel_id=1, source_target_pairs={{0,1},{1,2},{2,3},{3,4},{4,5},{5,6},{6,7},{7,0},{8,9},{9,10},{10,1... | collective-permute-start | bytes 3538952 | tf_op jit(solution)/shard_map/while/body/eval_jaxpr/ppermute | solution.py:132
  804.6 61.9 %collective-permute-start.7 = (f32[6,384,1,256]{3,1,0,2:T(8,128)}, f32[6,384,1,256]{3,1,0,2:T(8,128)}, u32[]{:S(2)}, u32[]{:S(2)}) collective-permute-start(f32[6,384,1,256]{3,1,0,2:T(8,128)} %get-tuple-element.505), channel_id=1, source_target_pairs={{0,1},{1,2},{2,3},{3,4},{4,5},{5,6},{6,7},{7,0},{8,9},{9,10},{10,1... | collective-permute-start | bytes 7077896 | tf_op jit(solution)/shard_map/while/body/eval_jaxpr/ppermute | solution.py:132
  806.2 49.5 %collective-permute-start.5 = (s32[384]{0:T(512)S(1)}, s32[384]{0:T(512)S(1)}, u32[]{:S(2)}, u32[]{:S(2)}) collective-permute-start(s32[384]{0:T(512)S(1)} %get-tuple-element.503), channel_id=1, source_target_pairs={{0,1},{1,2},{2,3},{3,4},{4,5},{5,6},{6,7},{7,0},{8,9},{9,10},{10,1... | collective-permute-start | bytes 4616 | tf_op jit(solution)/shard_map/while/body/eval_jaxpr/ppermute | solution.py:132
  806.2 74.7 %collective-permute-start.6 = (f32[6,384,1,256]{3,1,0,2:T(8,128)}, f32[6,384,1,256]{3,1,0,2:T(8,128)}, u32[]{:S(2)}, u32[]{:S(2)}) collective-permute-start(f32[6,384,1,256]{3,1,0,2:T(8,128)} %get-tuple-element.504), channel_id=1, source_target_pairs={{0,1},{1,2},{2,3},{3,4},{4,5},{5,6},{6,7},{7,0},{8,9},{9,10},{10,1... | collective-permute-start | bytes 7077896 | tf_op jit(solution)/shard_map/while/body/eval_jaxpr/ppermute | solution.py:132
  886.3 53.7 %collective-permute-start.3 = (bf16[6,384,1,256]{3,1,0,2:T(8,128)(2,1)}, bf16[6,384,1,256]{3,1,0,2:T(8,128)(2,1)S(1)}, u32[]{:S(2)}, u32[]{:S(2)}) collective-permute-start(bf16[6,384,1,256]{3,1,0,2:T(8,128)(2,1)} %get-tuple-element.501), channel_id=1, source_target_pairs={{0,1},{1,2},{2,3},{3,4},{4,5},{5,6},{6,7},{7,0},{8,9},{9,10},{10,1... | collective-permute-start | bytes 3538952 | tf_op jit(solution)/shard_map/while/body/eval_jaxpr/ppermute | solution.py:132
  888.8 53.4 %collective-permute-start.4 = (bf16[6,384,1,256]{3,1,0,2:T(8,128)(2,1)}, bf16[6,384,1,256]{3,1,0,2:T(8,128)(2,1)}, u32[]{:S(2)}, u32[]{:S(2)}) collective-permute-start(bf16[6,384,1,256]{3,1,0,2:T(8,128)(2,1)} %get-tuple-element.502), channel_id=1, source_target_pairs={{0,1},{1,2},{2,3},{3,4},{4,5},{5,6},{6,7},{7,0},{8,9},{9,10},{10,1... | collective-permute-start | bytes 3538952 | tf_op jit(solution)/shard_map/while/body/eval_jaxpr/ppermute | solution.py:132
  888.8 61.9 %collective-permute-start.7 = (f32[6,384,1,256]{3,1,0,2:T(8,128)}, f32[6,384,1,256]{3,1,0,2:T(8,128)}, u32[]{:S(2)}, u32[]{:S(2)}) collective-permute-start(f32[6,384,1,256]{3,1,0,2:T(8,128)} %get-tuple-element.505), channel_id=1, source_target_pairs={{0,1},{1,2},{2,3},{3,4},{4,5},{5,6},{6,7},{7,0},{8,9},{9,10},{10,1... | collective-permute-start | bytes 7077896 | tf_op jit(solution)/shard_map/while/body/eval_jaxpr/ppermute | solution.py:132
  890.4 49.5 %collective-permute-start.5 = (s32[384]{0:T(512)S(1)}, s32[384]{0:T(512)S(1)}, u32[]{:S(2)}, u32[]{:S(2)}) collective-permute-start(s32[384]{0:T(512)S(1)} %get-tuple-element.503), channel_id=1, source_target_pairs={{0,1},{1,2},{2,3},{3,4},{4,5},{5,6},{6,7},{7,0},{8,9},{9,10},{10,1... | collective-permute-start | bytes 4616 | tf_op jit(solution)/shard_map/while/body/eval_jaxpr/ppermute | solution.py:132
  890.4 74.7 %collective-permute-start.6 = (f32[6,384,1,256]{3,1,0,2:T(8,128)}, f32[6,384,1,256]{3,1,0,2:T(8,128)}, u32[]{:S(2)}, u32[]{:S(2)}) collective-permute-start(f32[6,384,1,256]{3,1,0,2:T(8,128)} %get-tuple-element.504), channel_id=1, source_target_pairs={{0,1},{1,2},{2,3},{3,4},{4,5},{5,6},{6,7},{7,0},{8,9},{9,10},{10,1... | collective-permute-start | bytes 7077896 | tf_op jit(solution)/shard_map/while/body/eval_jaxpr/ppermute | solution.py:132
  970.5 53.7 %collective-permute-start.3 = (bf16[6,384,1,256]{3,1,0,2:T(8,128)(2,1)}, bf16[6,384,1,256]{3,1,0,2:T(8,128)(2,1)S(1)}, u32[]{:S(2)}, u32[]{:S(2)}) collective-permute-start(bf16[6,384,1,256]{3,1,0,2:T(8,128)(2,1)} %get-tuple-element.501), channel_id=1, source_target_pairs={{0,1},{1,2},{2,3},{3,4},{4,5},{5,6},{6,7},{7,0},{8,9},{9,10},{10,1... | collective-permute-start | bytes 3538952 | tf_op jit(solution)/shard_map/while/body/eval_jaxpr/ppermute | solution.py:132
  973.0 53.4 %collective-permute-start.4 = (bf16[6,384,1,256]{3,1,0,2:T(8,128)(2,1)}, bf16[6,384,1,256]{3,1,0,2:T(8,128)(2,1)}, u32[]{:S(2)}, u32[]{:S(2)}) collective-permute-start(bf16[6,384,1,256]{3,1,0,2:T(8,128)(2,1)} %get-tuple-element.502), channel_id=1, source_target_pairs={{0,1},{1,2},{2,3},{3,4},{4,5},{5,6},{6,7},{7,0},{8,9},{9,10},{10,1... | collective-permute-start | bytes 3538952 | tf_op jit(solution)/shard_map/while/body/eval_jaxpr/ppermute | solution.py:132
  973.1 61.9 %collective-permute-start.7 = (f32[6,384,1,256]{3,1,0,2:T(8,128)}, f32[6,384,1,256]{3,1,0,2:T(8,128)}, u32[]{:S(2)}, u32[]{:S(2)}) collective-permute-start(f32[6,384,1,256]{3,1,0,2:T(8,128)} %get-tuple-element.505), channel_id=1, source_target_pairs={{0,1},{1,2},{2,3},{3,4},{4,5},{5,6},{6,7},{7,0},{8,9},{9,10},{10,1... | collective-permute-start | bytes 7077896 | tf_op jit(solution)/shard_map/while/body/eval_jaxpr/ppermute | solution.py:132
  974.6 49.5 %collective-permute-start.5 = (s32[384]{0:T(512)S(1)}, s32[384]{0:T(512)S(1)}, u32[]{:S(2)}, u32[]{:S(2)}) collective-permute-start(s32[384]{0:T(512)S(1)} %get-tuple-element.503), channel_id=1, source_target_pairs={{0,1},{1,2},{2,3},{3,4},{4,5},{5,6},{6,7},{7,0},{8,9},{9,10},{10,1... | collective-permute-start | bytes 4616 | tf_op jit(solution)/shard_map/while/body/eval_jaxpr/ppermute | solution.py:132
  974.7 74.7 %collective-permute-start.6 = (f32[6,384,1,256]{3,1,0,2:T(8,128)}, f32[6,384,1,256]{3,1,0,2:T(8,128)}, u32[]{:S(2)}, u32[]{:S(2)}) collective-permute-start(f32[6,384,1,256]{3,1,0,2:T(8,128)} %get-tuple-element.504), channel_id=1, source_target_pairs={{0,1},{1,2},{2,3},{3,4},{4,5},{5,6},{6,7},{7,0},{8,9},{9,10},{10,1... | collective-permute-start | bytes 7077896 | tf_op jit(solution)/shard_map/while/body/eval_jaxpr/ppermute | solution.py:132
  1054.8 53.7 %collective-permute-start.3 = (bf16[6,384,1,256]{3,1,0,2:T(8,128)(2,1)}, bf16[6,384,1,256]{3,1,0,2:T(8,128)(2,1)S(1)}, u32[]{:S(2)}, u32[]{:S(2)}) collective-permute-start(bf16[6,384,1,256]{3,1,0,2:T(8,128)(2,1)} %get-tuple-element.501), channel_id=1, source_target_pairs={{0,1},{1,2},{2,3},{3,4},{4,5},{5,6},{6,7},{7,0},{8,9},{9,10},{10,1... | collective-permute-start | bytes 3538952 | tf_op jit(solution)/shard_map/while/body/eval_jaxpr/ppermute | solution.py:132
  1057.3 53.4 %collective-permute-start.4 = (bf16[6,384,1,256]{3,1,0,2:T(8,128)(2,1)}, bf16[6,384,1,256]{3,1,0,2:T(8,128)(2,1)}, u32[]{:S(2)}, u32[]{:S(2)}) collective-permute-start(bf16[6,384,1,256]{3,1,0,2:T(8,128)(2,1)} %get-tuple-element.502), channel_id=1, source_target_pairs={{0,1},{1,2},{2,3},{3,4},{4,5},{5,6},{6,7},{7,0},{8,9},{9,10},{10,1... | collective-permute-start | bytes 3538952 | tf_op jit(solution)/shard_map/while/body/eval_jaxpr/ppermute | solution.py:132
  1057.3 61.9 %collective-permute-start.7 = (f32[6,384,1,256]{3,1,0,2:T(8,128)}, f32[6,384,1,256]{3,1,0,2:T(8,128)}, u32[]{:S(2)}, u32[]{:S(2)}) collective-permute-start(f32[6,384,1,256]{3,1,0,2:T(8,128)} %get-tuple-element.505), channel_id=1, source_target_pairs={{0,1},{1,2},{2,3},{3,4},{4,5},{5,6},{6,7},{7,0},{8,9},{9,10},{10,1... | collective-permute-start | bytes 7077896 | tf_op jit(solution)/shard_map/while/body/eval_jaxpr/ppermute | solution.py:132
  1058.9 49.5 %collective-permute-start.5 = (s32[384]{0:T(512)S(1)}, s32[384]{0:T(512)S(1)}, u32[]{:S(2)}, u32[]{:S(2)}) collective-permute-start(s32[384]{0:T(512)S(1)} %get-tuple-element.503), channel_id=1, source_target_pairs={{0,1},{1,2},{2,3},{3,4},{4,5},{5,6},{6,7},{7,0},{8,9},{9,10},{10,1... | collective-permute-start | bytes 4616 | tf_op jit(solution)/shard_map/while/body/eval_jaxpr/ppermute | solution.py:132
  1058.9 74.7 %collective-permute-start.6 = (f32[6,384,1,256]{3,1,0,2:T(8,128)}, f32[6,384,1,256]{3,1,0,2:T(8,128)}, u32[]{:S(2)}, u32[]{:S(2)}) collective-permute-start(f32[6,384,1,256]{3,1,0,2:T(8,128)} %get-tuple-element.504), channel_id=1, source_target_pairs={{0,1},{1,2},{2,3},{3,4},{4,5},{5,6},{6,7},{7,0},{8,9},{9,10},{10,1... | collective-permute-start | bytes 7077896 | tf_op jit(solution)/shard_map/while/body/eval_jaxpr/ppermute | solution.py:132
  1139.0 53.7 %collective-permute-start.3 = (bf16[6,384,1,256]{3,1,0,2:T(8,128)(2,1)}, bf16[6,384,1,256]{3,1,0,2:T(8,128)(2,1)S(1)}, u32[]{:S(2)}, u32[]{:S(2)}) collective-permute-start(bf16[6,384,1,256]{3,1,0,2:T(8,128)(2,1)} %get-tuple-element.501), channel_id=1, source_target_pairs={{0,1},{1,2},{2,3},{3,4},{4,5},{5,6},{6,7},{7,0},{8,9},{9,10},{10,1... | collective-permute-start | bytes 3538952 | tf_op jit(solution)/shard_map/while/body/eval_jaxpr/ppermute | solution.py:132
  1141.5 53.4 %collective-permute-start.4 = (bf16[6,384,1,256]{3,1,0,2:T(8,128)(2,1)}, bf16[6,384,1,256]{3,1,0,2:T(8,128)(2,1)}, u32[]{:S(2)}, u32[]{:S(2)}) collective-permute-start(bf16[6,384,1,256]{3,1,0,2:T(8,128)(2,1)} %get-tuple-element.502), channel_id=1, source_target_pairs={{0,1},{1,2},{2,3},{3,4},{4,5},{5,6},{6,7},{7,0},{8,9},{9,10},{10,1... | collective-permute-start | bytes 3538952 | tf_op jit(solution)/shard_map/while/body/eval_jaxpr/ppermute | solution.py:132
  1141.5 61.9 %collective-permute-start.7 = (f32[6,384,1,256]{3,1,0,2:T(8,128)}, f32[6,384,1,256]{3,1,0,2:T(8,128)}, u32[]{:S(2)}, u32[]{:S(2)}) collective-permute-start(f32[6,384,1,256]{3,1,0,2:T(8,128)} %get-tuple-element.505), channel_id=1, source_target_pairs={{0,1},{1,2},{2,3},{3,4},{4,5},{5,6},{6,7},{7,0},{8,9},{9,10},{10,1... | collective-permute-start | bytes 7077896 | tf_op jit(solution)/shard_map/while/body/eval_jaxpr/ppermute | solution.py:132
  1143.1 49.5 %collective-permute-start.5 = (s32[384]{0:T(512)S(1)}, s32[384]{0:T(512)S(1)}, u32[]{:S(2)}, u32[]{:S(2)}) collective-permute-start(s32[384]{0:T(512)S(1)} %get-tuple-element.503), channel_id=1, source_target_pairs={{0,1},{1,2},{2,3},{3,4},{4,5},{5,6},{6,7},{7,0},{8,9},{9,10},{10,1... | collective-permute-start | bytes 4616 | tf_op jit(solution)/shard_map/while/body/eval_jaxpr/ppermute | solution.py:132
  1143.1 74.7 %collective-permute-start.6 = (f32[6,384,1,256]{3,1,0,2:T(8,128)}, f32[6,384,1,256]{3,1,0,2:T(8,128)}, u32[]{:S(2)}, u32[]{:S(2)}) collective-permute-start(f32[6,384,1,256]{3,1,0,2:T(8,128)} %get-tuple-element.504), channel_id=1, source_target_pairs={{0,1},{1,2},{2,3},{3,4},{4,5},{5,6},{6,7},{7,0},{8,9},{9,10},{10,1... | collective-permute-start | bytes 7077896 | tf_op jit(solution)/shard_map/while/body/eval_jaxpr/ppermute | solution.py:132
  1223.2 53.7 %collective-permute-start.3 = (bf16[6,384,1,256]{3,1,0,2:T(8,128)(2,1)}, bf16[6,384,1,256]{3,1,0,2:T(8,128)(2,1)S(1)}, u32[]{:S(2)}, u32[]{:S(2)}) collective-permute-start(bf16[6,384,1,256]{3,1,0,2:T(8,128)(2,1)} %get-tuple-element.501), channel_id=1, source_target_pairs={{0,1},{1,2},{2,3},{3,4},{4,5},{5,6},{6,7},{7,0},{8,9},{9,10},{10,1... | collective-permute-start | bytes 3538952 | tf_op jit(solution)/shard_map/while/body/eval_jaxpr/ppermute | solution.py:132
  1225.7 53.4 %collective-permute-start.4 = (bf16[6,384,1,256]{3,1,0,2:T(8,128)(2,1)}, bf16[6,384,1,256]{3,1,0,2:T(8,128)(2,1)}, u32[]{:S(2)}, u32[]{:S(2)}) collective-permute-start(bf16[6,384,1,256]{3,1,0,2:T(8,128)(2,1)} %get-tuple-element.502), channel_id=1, source_target_pairs={{0,1},{1,2},{2,3},{3,4},{4,5},{5,6},{6,7},{7,0},{8,9},{9,10},{10,1... | collective-permute-start | bytes 3538952 | tf_op jit(solution)/shard_map/while/body/eval_jaxpr/ppermute | solution.py:132
  1225.7 61.9 %collective-permute-start.7 = (f32[6,384,1,256]{3,1,0,2:T(8,128)}, f32[6,384,1,256]{3,1,0,2:T(8,128)}, u32[]{:S(2)}, u32[]{:S(2)}) collective-permute-start(f32[6,384,1,256]{3,1,0,2:T(8,128)} %get-tuple-element.505), channel_id=1, source_target_pairs={{0,1},{1,2},{2,3},{3,4},{4,5},{5,6},{6,7},{7,0},{8,9},{9,10},{10,1... | collective-permute-start | bytes 7077896 | tf_op jit(solution)/shard_map/while/body/eval_jaxpr/ppermute | solution.py:132
  1227.3 49.5 %collective-permute-start.5 = (s32[384]{0:T(512)S(1)}, s32[384]{0:T(512)S(1)}, u32[]{:S(2)}, u32[]{:S(2)}) collective-permute-start(s32[384]{0:T(512)S(1)} %get-tuple-element.503), channel_id=1, source_target_pairs={{0,1},{1,2},{2,3},{3,4},{4,5},{5,6},{6,7},{7,0},{8,9},{9,10},{10,1... | collective-permute-start | bytes 4616 | tf_op jit(solution)/shard_map/while/body/eval_jaxpr/ppermute | solution.py:132
  1227.3 74.7 %collective-permute-start.6 = (f32[6,384,1,256]{3,1,0,2:T(8,128)}, f32[6,384,1,256]{3,1,0,2:T(8,128)}, u32[]{:S(2)}, u32[]{:S(2)}) collective-permute-start(f32[6,384,1,256]{3,1,0,2:T(8,128)} %get-tuple-element.504), channel_id=1, source_target_pairs={{0,1},{1,2},{2,3},{3,4},{4,5},{5,6},{6,7},{7,0},{8,9},{9,10},{10,1... | collective-permute-start | bytes 7077896 | tf_op jit(solution)/shard_map/while/body/eval_jaxpr/ppermute | solution.py:132
  1307.4 53.7 %collective-permute-start.3 = (bf16[6,384,1,256]{3,1,0,2:T(8,128)(2,1)}, bf16[6,384,1,256]{3,1,0,2:T(8,128)(2,1)S(1)}, u32[]{:S(2)}, u32[]{:S(2)}) collective-permute-start(bf16[6,384,1,256]{3,1,0,2:T(8,128)(2,1)} %get-tuple-element.501), channel_id=1, source_target_pairs={{0,1},{1,2},{2,3},{3,4},{4,5},{5,6},{6,7},{7,0},{8,9},{9,10},{10,1... | collective-permute-start | bytes 3538952 | tf_op jit(solution)/shard_map/while/body/eval_jaxpr/ppermute | solution.py:132
  1309.9 53.4 %collective-permute-start.4 = (bf16[6,384,1,256]{3,1,0,2:T(8,128)(2,1)}, bf16[6,384,1,256]{3,1,0,2:T(8,128)(2,1)}, u32[]{:S(2)}, u32[]{:S(2)}) collective-permute-start(bf16[6,384,1,256]{3,1,0,2:T(8,128)(2,1)} %get-tuple-element.502), channel_id=1, source_target_pairs={{0,1},{1,2},{2,3},{3,4},{4,5},{5,6},{6,7},{7,0},{8,9},{9,10},{10,1... | collective-permute-start | bytes 3538952 | tf_op jit(solution)/shard_map/while/body/eval_jaxpr/ppermute | solution.py:132
  1309.9 61.9 %collective-permute-start.7 = (f32[6,384,1,256]{3,1,0,2:T(8,128)}, f32[6,384,1,256]{3,1,0,2:T(8,128)}, u32[]{:S(2)}, u32[]{:S(2)}) collective-permute-start(f32[6,384,1,256]{3,1,0,2:T(8,128)} %get-tuple-element.505), channel_id=1, source_target_pairs={{0,1},{1,2},{2,3},{3,4},{4,5},{5,6},{6,7},{7,0},{8,9},{9,10},{10,1... | collective-permute-start | bytes 7077896 | tf_op jit(solution)/shard_map/while/body/eval_jaxpr/ppermute | solution.py:132
  1311.5 49.5 %collective-permute-start.5 = (s32[384]{0:T(512)S(1)}, s32[384]{0:T(512)S(1)}, u32[]{:S(2)}, u32[]{:S(2)}) collective-permute-start(s32[384]{0:T(512)S(1)} %get-tuple-element.503), channel_id=1, source_target_pairs={{0,1},{1,2},{2,3},{3,4},{4,5},{5,6},{6,7},{7,0},{8,9},{9,10},{10,1... | collective-permute-start | bytes 4616 | tf_op jit(solution)/shard_map/while/body/eval_jaxpr/ppermute | solution.py:132
  1311.5 74.7 %collective-permute-start.6 = (f32[6,384,1,256]{3,1,0,2:T(8,128)}, f32[6,384,1,256]{3,1,0,2:T(8,128)}, u32[]{:S(2)}, u32[]{:S(2)}) collective-permute-start(f32[6,384,1,256]{3,1,0,2:T(8,128)} %get-tuple-element.504), channel_id=1, source_target_pairs={{0,1},{1,2},{2,3},{3,4},{4,5},{5,6},{6,7},{7,0},{8,9},{9,10},{10,1... | collective-permute-start | bytes 7077896 | tf_op jit(solution)/shard_map/while/body/eval_jaxpr/ppermute | solution.py:132
  1397.8 43.9 %collective-permute-start.8 = (f32[6,384,1,256]{1,3,0,2:T(8,128)}, f32[6,384,1,256]{1,3,0,2:T(8,128)}, u32[]{:S(2)}, u32[]{:S(2)}) collective-permute-start(f32[6,384,1,256]{1,3,0,2:T(8,128)} %copy.182), channel_id=1, source_target_pairs={{0,1},{1,2},{2,3},{3,4},{4,5},{5,6},{6,7},{7,0},{8,9},{9,10},{10,1... | collective-permute-start | bytes 7077896 | tf_op jit(solution)/shard_map/ppermute | solution.py:137
  1411.1 43.2 %collective-permute-start.9 = (bf16[6,384,1,256]{3,1,0,2:T(8,128)(2,1)}, bf16[6,384,1,256]{3,1,0,2:T(8,128)(2,1)}, u32[]{:S(2)}, u32[]{:S(2)}) collective-permute-start(bf16[6,384,1,256]{3,1,0,2:T(8,128)(2,1)} %convert.37), channel_id=1, source_target_pairs={{0,1},{1,2},{2,3},{3,4},{4,5},{5,6},{6,7},{7,0},{8,9},{9,10},{10,1... | collective-permute-start | bytes 3538952 | tf_op jit(solution)/shard_map/ppermute | solution.py:137
  1477.2 526.9 %all-reduce.11.cloned.1.call-start = ((), (), s32[]{:S(2)}) async-start(), calls=%async_computation.2 | async-start | bytes 28311552 | tf_op jit(solution)/shard_map/psum | solution.py:145
  (180 other events, 2630.7 us)
Sparse Core Ops, SparseCore 0:
  348.9 371.0 all-reduce.6
  1477.3 369.8 all-reduce.8
  1850.4 153.6 all-reduce.10
where the time goes:
time: 2030 us; the launch traced here: 2020 us
  waiting for transfers between devices  1250 us (62%)
  matrix products  310 us (15%)
  local copies, waits for them, and re-layouts  168 us (8%)
  other arithmetic  134 us (7%)
  blocking collectives  78.2 us (4%)
  starting transfers between devices  69.8 us (3%)
    ppermute x35, waiting for transfers between devices, bwd_step(): lax.ppermute((k_blk, v_blk, k_pos, dk_run, dv_run), 'cp', next_hop)  395 us
    psum x1, waiting for transfers between devices, per_device(): lax.psum(jnp.einsum('bkgqd,kgdm->bqm', out_bf, wo_split, preferred_elemen...  357 us
    psum x1, waiting for transfers between devices, per_device(): lax.psum(jnp.einsum('bsh,dh->bsd', dq_bf, w_q, preferred_element_type=jnp...  280 us
    ppermute x21, waiting for transfers between devices, fwd_step(): k_blk, v_blk, k_pos = lax.ppermute((k_blk, v_blk, k_pos), 'cp', next_hop)  112 us
    psum x1, waiting for transfers between devices, per_device(): lax.psum(jnp.einsum('bsd,bsh->dh', normed, dq_bf, preferred_element_type=...  101 us
    while x245, local copies, waits for them, and re-layouts  76.7 us
    psum x1, blocking collectives, per_device(): d_qnorm = lax.psum(dq_gain, ('tp', 'cp'))  54.2 us
    dot_general x8, matrix products, grad_block(): jnp.einsum('bkgqs,bkgqd->bskd', attn_prob.astype(jnp.bfloat16), d_out, pr...  46 us
  transfers between devices with their start and end apart: 61, of which 31 were waited for; matrix products, arithmetic and copies ran while one was open for 15% of the time, Pallas kernels for 0%

commit v1 on v0

v1 whole, which is shorter than its diff:
```python
import functools
import math

import jax
import jax.numpy as jnp
from jax import lax
from jax.experimental import pallas as pl
from jax.experimental.pallas import tpu as pltpu
from jax.sharding import Mesh, PartitionSpec as P


EPS = 1e-6
ROPE_BASE = 1000000.0
ROPE_SCALE = 8.0
NEG_BIG = -1e30
LOG2E = math.log2(math.e)
VMEM_LIMIT = 60 * 1024 * 1024
BF = jnp.bfloat16
F32 = jnp.float32


def dot_nn(a, b):
    return lax.dot_general(a, b, (((1,), (0,)), ((), ())), preferred_element_type=F32)


def dot_nt(a, b):
    return lax.dot_general(a, b, (((1,), (1,)), ((), ())), preferred_element_type=F32)


def rms_inv(values):
    return lax.rsqrt(jnp.mean(values * values, axis=-1, keepdims=True) + EPS)


def rope_apply(values, cos_t, sin_t):
    half = values.shape[-1] // 2
    lo, hi = values[:, :half], values[:, half:]
    return jnp.concatenate([lo * cos_t - hi * sin_t, hi * cos_t + lo * sin_t], axis=-1)


def rope_back(values, cos_t, sin_t):
    half = values.shape[-1] // 2
    lo, hi = values[:, :half], values[:, half:]
    return jnp.concatenate([lo * cos_t + hi * sin_t, hi * cos_t - lo * sin_t], axis=-1)


def head_norm(raw_bf, gain, cos_t, sin_t):
    raw = raw_bf.astype(F32)
    return rope_apply(raw * rms_inv(raw) * (1.0 + gain), cos_t, sin_t).astype(BF)


def head_norm_back(grad, raw_bf, gain, cos_t, sin_t):
    raw = raw_bf.astype(F32)
    inv = rms_inv(raw)
    unit = raw * inv
    d_scaled = rope_back(grad, cos_t, sin_t)
    d_gain = jnp.sum(d_scaled * unit, axis=0, keepdims=True)
    d_unit = d_scaled * (1.0 + gain)
    d_raw = inv * (d_unit - unit * jnp.mean(d_unit * unit, axis=-1, keepdims=True))
    return d_raw.astype(BF), d_gain


def pre_body(x_ref, wq_ref, wk_ref, wv_ref, pre_ref, qg_ref, kg_ref, cos_ref, sin_ref, normed_ref, qraw_ref, kraw_ref, qfin_ref, kv_ref):
    hd = qg_ref.shape[1]
    x = x_ref[0].astype(F32)
    n = (x * rms_inv(x) * (1.0 + pre_ref[...])).astype(BF)
    normed_ref[0] = n
    cos_t, sin_t = cos_ref[...], sin_ref[...]
    kraw = dot_nn(n, wk_ref[...]).astype(BF)
    kraw_ref[0] = kraw
    kv_ref[0, :, :hd] = head_norm(kraw, kg_ref[...], cos_t, sin_t)
    kv_ref[0, :, hd:] = dot_nn(n, wv_ref[...]).astype(BF)
    qraw = dot_nn(n, wq_ref[...]).astype(BF)
    qraw_ref[0] = qraw
    for h in range(qraw.shape[1] // hd):
        cols = slice(h * hd, (h + 1) * hd)
        qfin_ref[0, :, cols] = head_norm(qraw[:, cols], qg_ref[...], cos_t, sin_t)


def const_spec(shape):
    return pl.BlockSpec(shape, lambda *_: (0,) * len(shape), pipeline_mode=pl.Buffered(1))


def params(sem=("arbitrary",)):
    return pltpu.CompilerParams(dimension_semantics=sem, vmem_limit_bytes=VMEM_LIMIT)


def pre_call(off, nb, hidden, w_q, w_k, w_v, w_pre, q_norm, k_norm, cos_t, sin_t):
    _, s, d = hidden.shape
    dq, dk = w_q.shape[1], w_k.shape[1]
    row = lambda width: pl.BlockSpec((1, s, width), lambda b: (b, 0, 0))
    shape = lambda width: jax.ShapeDtypeStruct((nb, s, width), BF)
    return pl.pallas_call(
        pre_body,
        grid=(nb,),
        in_specs=[pl.BlockSpec((1, s, d), lambda b: (b + off, 0, 0)), const_spec(w_q.shape), const_spec(w_k.shape), const_spec(w_v.shape), const_spec(w_pre.shape), const_spec(q_norm.shape), const_spec(k_norm.shape), const_spec(cos_t.shape), const_spec(sin_t.shape)],
        out_specs=[row(d), row(dq), row(dk), row(dq), row(2 * dk)],
        out_shape=[shape(d), shape(dq), shape(dk), shape(dq), shape(2 * dk)],
        compiler_params=params(),
        cost_estimate=pl.CostEstimate(flops=2 * nb * s * d * (dq + 2 * dk), bytes_accessed=4 * nb * s * d, transcendentals=0),
        name="pre",
    )(hidden, w_q, w_k, w_v, w_pre, q_norm, k_norm, cos_t, sin_t)


def seq_copies(src, buf, sem, b, slot, piece):
    owners = src.shape[0]
    out = []
    for o in range(owners):
        for half, p in ((0, o), (1, 2 * owners - 1 - o)):
            out.append(pltpu.make_async_copy(src.at[o, b, pl.ds(half * piece, piece)], buf.at[slot, pl.ds(p * piece, piece)], sem.at[slot]))
    return out


def stream(pairs, b, nb, piece):
    slot = lax.rem(b, 2)

    @pl.when(b == 0)
    def _():
        for src, buf, sem in pairs:
            for cp in seq_copies(src, buf, sem, 0, 0, piece):
                cp.start()

    for src, buf, sem in pairs:
        for cp in seq_copies(src, buf, sem, b, slot, piece):
            cp.wait()

    @pl.when(b + 1 < nb)
    def _():
        for src, buf, sem in pairs:
            for cp in seq_copies(src, buf, sem, b + 1, 1 - slot, piece):
                cp.start()

    return slot


def fwd_body(nb, owners, hd, c_ref, q_ref, kv_ref, o_ref, of_ref, lse_ref, buf, sem, acc_ref, m_ref, l_ref):
    b = pl.program_id(0)
    piece = q_ref.shape[1] // 2
    blk = 4 * piece
    heads = q_ref.shape[2] // hd
    factor = hd ** -0.5 * LOG2E
    slot = stream([(kv_ref, buf, sem)], b, nb, piece)
    c = c_ref[0]
    for half in (0, 1):
        p = c if half == 0 else 2 * owners - 1 - c
        last = p // 4
        shift = (p - 4 * last) * piece
        rows = slice(half * piece, (half + 1) * piece)

        def keys(j):
            base = pl.multiple_of(j * blk, blk)
            return buf[slot, pl.ds(base, blk), :hd], buf[slot, pl.ds(base, blk), hd:]

        k_blk, v_blk = keys(last)
        for h in range(heads):
            s2 = dot_nt(q_ref[0, rows, h * hd:(h + 1) * hd], k_blk) * factor
            gap = lax.broadcasted_iota(jnp.int32, s2.shape, 1) - lax.broadcasted_iota(jnp.int32, s2.shape, 0)
            s2 = jnp.where(gap <= shift, s2, NEG_BIG)
            m = jnp.max(s2, axis=1, keepdims=True)
            prob = jnp.exp2(s2 - m)
            m_ref[h] = m
            l_ref[h] = jnp.sum(prob, axis=1, keepdims=True)
            acc_ref[h] = dot_nn(prob.astype(BF), v_blk)

        def step(j, carry):
            k_blk, v_blk = keys(j)
            for h in range(heads):
                s2 = dot_nt(q_ref[0, rows, h * hd:(h + 1) * hd], k_blk) * factor
                m_old = m_ref[h]
                m = jnp.maximum(m_old, jnp.max(s2, axis=1, keepdims=True))
                prob = jnp.exp2(s2 - m)
                alpha = jnp.exp2(m_old - m)
                m_ref[h] = m
                l_ref[h] = l_ref[h] * alpha + jnp.sum(prob, axis=1, keepdims=True)
                acc_ref[h] = acc_ref[h] * alpha + dot_nn(prob.astype(BF), v_blk)
            return carry

        lax.fori_loop(0, last, step, 0)
        for h in range(heads):
            out = acc_ref[h] / l_ref[h]
            cols = slice(h * hd, (h + 1) * hd)
            of_ref[0, rows, cols] = out
            o_ref[0, rows, cols] = out.astype(BF)
            lse_ref[0, rows, h:h + 1] = m_ref[h] + jnp.log2(l_ref[h])


def fwd_call(c_arr, q_fin, kv_all, hd):
    nb, s, dq = q_fin.shape
    owners = kv_all.shape[0]
    heads = dq // hd
    piece = s // 2
    row = lambda width: pl.BlockSpec((1, s, width), lambda b: (b, 0, 0))
    return pl.pallas_call(
        functools.partial(fwd_body, nb, owners, hd),
        grid=(nb,),
        in_specs=[pl.BlockSpec(memory_space=pltpu.SMEM), row(dq), pl.BlockSpec(memory_space=pl.ANY)],
        out_specs=[row(dq), row(dq), row(heads)],
        out_shape=[jax.ShapeDtypeStruct((nb, s, dq), BF), jax.ShapeDtypeStruct((nb, s, dq), F32), jax.ShapeDtypeStruct((nb, s, heads), F32)],
        scratch_shapes=[pltpu.VMEM((2, owners * s, kv_all.shape[3]), BF), pltpu.SemaphoreType.DMA((2,)), pltpu.VMEM((heads, piece, hd), F32), pltpu.VMEM((heads, piece, 1), F32), pltpu.VMEM((heads, piece, 1), F32)],
        compiler_params=params(),
        cost_estimate=pl.CostEstimate(flops=2 * nb * s * owners * s * dq, bytes_accessed=2 * kv_all.size, transcendentals=nb * s * owners * s // 2),
        name="attend",
    )(c_arr, q_fin, kv_all)


def mid_body(hd, t_ref, o0_ref, o1_ref, o2_ref, o3_ref, of_ref, x_ref, gy_ref, wfull_ref, wo_ref, post_ref, *rest):
    y_ref, dattn_ref, dout_ref, delta_ref, dpost_ref, ocat_ref = rest[-6:]
    first = jnp.logical_and(pl.program_id(0) == 0, pl.program_id(1) == 0)
    dq = o0_ref.shape[2]
    for i, ref in enumerate((o0_ref, o1_ref, o2_ref, o3_ref)):
        ocat_ref[:, pl.ds(pl.multiple_of(t_ref[i] * dq, dq), dq)] = ref[0]
    attn = dot_nn(ocat_ref[...], wfull_ref[...])
    inv = rms_inv(attn)
    unit = attn * inv
    gain = 1.0 + post_ref[...]
    y_ref[0] = (x_ref[0].astype(F32) + unit * gain).astype(BF)
    gy = gy_ref[0].astype(F32)
    part = jnp.sum(gy * unit, axis=0, keepdims=True)

    @pl.when(first)
    def _():
        dpost_ref[...] = part

    @pl.when(jnp.logical_not(first))
    def _():
        dpost_ref[...] += part

    d_unit = gy * gain
    d_attn = (inv * (d_unit - unit * jnp.mean(d_unit * unit, axis=-1, keepdims=True))).astype(BF)
    dattn_ref[0] = d_attn
    d_out = dot_nt(d_attn, wo_ref[...]).astype(BF)
    dout_ref[0] = d_out
    prod = d_out.astype(F32) * of_ref[0]
    for h in range(dq // hd):
        delta_ref[0, :, h:h + 1] = jnp.sum(prod[:, h * hd:(h + 1) * hd], axis=1, keepdims=True)


def mid_call(off, nb, hd, t_arr, o_blocks, o_f32, hidden, cotangent, w_full, w_o, w_post, carried):
    batch, s, d = hidden.shape
    dq = o_f32.shape[2]
    tile = s // 2
    loc = lambda width: pl.BlockSpec((1, tile, width), lambda b, i: (b, i, 0))
    full = lambda width: pl.BlockSpec((1, tile, width), lambda b, i: (b + off, i, 0))
    ins = [t_arr, *o_blocks, o_f32, hidden, cotangent, w_full, w_o, w_post]
    in_specs = [pl.BlockSpec(memory_space=pltpu.SMEM)] + [loc(dq)] * 5 + [full(d), full(d), const_spec(w_full.shape), const_spec(w_o.shape), const_spec(w_post.shape)]
    aliases = {}
    if carried is not None:
        for i, arr in enumerate(carried):
            aliases[len(ins)] = i
            ins.append(arr)
            in_specs.append(pl.BlockSpec(memory_space=pl.ANY))
    return pl.pallas_call(
        functools.partial(mid_body, hd),
        grid=(nb, 2),
        in_specs=in_specs,
        out_specs=[full(d), full(d), loc(dq), loc(dq // hd), pl.BlockSpec((1, d), lambda b, i: (0, 0))],
        out_shape=[jax.ShapeDtypeStruct((batch, s, d), BF), jax.ShapeDtypeStruct((batch, s, d), BF), jax.ShapeDtypeStruct((nb, s, dq), BF), jax.ShapeDtypeStruct((nb, s, dq // hd), F32), jax.ShapeDtypeStruct((1, d), F32)],
        scratch_shapes=[pltpu.VMEM((tile, w_full.shape[0]), BF)],
        input_output_aliases=aliases,
        compiler_params=params(("arbitrary", "arbitrary")),
        cost_estimate=pl.CostEstimate(flops=2 * nb * s * d * (w_full.shape[0] + dq), bytes_accessed=10 * nb * s * d, transcendentals=0),
        name="mid",
    )(*ins)


def dq_body(nb, owners, hd, c_ref, q_ref, do_ref, lse_ref, delta_ref, qraw_ref, gain_ref, cos_ref, sin_ref, kv_ref, dq_ref, dgain_ref, buf, sem, acc_ref):
    b = pl.program_id(0)
    piece = q_ref.shape[1] // 2
    blk = 4 * piece
    heads = q_ref.shape[2] // hd
    scale = hd ** -0.5
    factor = scale * LOG2E
    slot = stream([(kv_ref, buf, sem)], b, nb, piece)
    c = c_ref[0]
    total = jnp.zeros((1, hd), F32)
    for half in (0, 1):
        p = c if half == 0 else 2 * owners - 1 - c
        last = p // 4
        shift = (p - 4 * last) * piece
        rows = slice(half * piece, (half + 1) * piece)

        def block(j, h, masked):
            base = pl.multiple_of(j * blk, blk)
            k_blk, v_blk = buf[slot, pl.ds(base, blk), :hd], buf[slot, pl.ds(base, blk), hd:]
            cols = slice(h * hd, (h + 1) * hd)
            s2 = dot_nt(q_ref[0, rows, cols], k_blk) * factor
            prob = jnp.exp2(s2 - lse_ref[0, rows, h:h + 1])
            if masked:
                gap = lax.broadcasted_iota(jnp.int32, s2.shape, 1) - lax.broadcasted_iota(jnp.int32, s2.shape, 0)
                prob = jnp.where(gap <= shift, prob, 0.0)
            d_prob = dot_nt(do_ref[0, rows, cols], v_blk)
            d_score = (prob * (d_prob - delta_ref[0, rows, h:h + 1]) * scale).astype(BF)
            return dot_nn(d_score, k_blk)

        for h in range(heads):
            acc_ref[h] = block(last, h, True)

        def step(j, carry):
            for h in range(heads):
                acc_ref[h] += block(j, h, False)
            return carry

        lax.fori_loop(0, last, step, 0)
        for h in range(heads):
            cols = slice(h * hd, (h + 1) * hd)
            d_raw, d_gain = head_norm_back(acc_ref[h], qraw_ref[0, rows, cols], gain_ref[...], cos_ref[rows, :], sin_ref[rows, :])
            dq_ref[0, rows, cols] = d_raw
            total = total + d_gain

    @pl.when(b == 0)
    def _():
        dgain_ref[...] = total

    @pl.when(b > 0)
    def _():
        dgain_ref[...] += total


def dq_call(c_arr, q_fin, d_out, lse, delta, q_raw, q_norm, cos_t, sin_t, kv_all, hd):
    nb, s, dq = q_fin.shape
    owners = kv_all.shape[0]
    heads = dq // hd
    piece = s // 2
    row = lambda width: pl.BlockSpec((1, s, width), lambda b: (b, 0, 0))
    return pl.pallas_call(
        functools.partial(dq_body, nb, owners, hd),
        grid=(nb,),
        in_specs=[pl.BlockSpec(memory_space=pltpu.SMEM), row(dq), row(dq), row(heads), row(heads), row(dq), const_spec(q_norm.shape), const_spec(cos_t.shape), const_spec(sin_t.shape), pl.BlockSpec(memory_space=pl.ANY)],
        out_specs=[row(dq), pl.BlockSpec((1, hd), lambda b: (0, 0))],
        out_shape=[jax.ShapeDtypeStruct((nb, s, dq), BF), jax.ShapeDtypeStruct((1, hd), F32)],
        scratch_shapes=[pltpu.VMEM((2, owners * s, kv_all.shape[3]), BF), pltpu.SemaphoreType.DMA((2,)), pltpu.VMEM((heads, piece, hd), F32)],
        compiler_params=params(),
        cost_estimate=pl.CostEstimate(flops=3 * nb * s * owners * s * dq, bytes_accessed=2 * kv_all.size, transcendentals=nb * s * owners * s // 2),
        name="grad_q",
    )(c_arr, q_fin, d_out, lse, delta, q_raw, q_norm, cos_t, sin_t, kv_all)


def dkv_body(nb, owners, hd, c_ref, kv_ref, stat_ref, kraw_ref, gain_ref, cos_ref, sin_ref, q_ref, do_ref, dkv_ref, dgain_ref, qbuf, dobuf, qsem, dosem, dk_ref, dv_ref):
    b = pl.program_id(0)
    piece = kv_ref.shape[1] // 2
    blk = 4 * piece
    n_blk = 2 * owners // 4
    heads = qbuf.shape[2] // hd
    scale = hd ** -0.5
    factor = scale * LOG2E
    slot = stream([(q_ref, qbuf, qsem), (do_ref, dobuf, dosem)], b, nb, piece)
    c = c_ref[0]
    total = jnp.zeros((1, hd), F32)
    for half in (0, 1):
        p = c if half == 0 else 2 * owners - 1 - c
        first = p // 4
        shift = (p - 4 * first) * piece
        rows = slice(half * piece, (half + 1) * piece)
        k_own, v_own = kv_ref[0, rows, :hd], kv_ref[0, rows, hd:]

        def block(j, masked):
            base = pl.multiple_of(j * blk, blk)
            dk_new, dv_new = None, None
            for h in range(heads):
                cols = slice(h * hd, (h + 1) * hd)
                q_blk, do_blk = qbuf[slot, pl.ds(base, blk), cols], dobuf[slot, pl.ds(base, blk), cols]
                s2 = dot_nt(k_own, q_blk) * factor
                prob = jnp.exp2(s2 - stat_ref[0, h:h + 1, pl.ds(base, blk)])
                if masked:
                    gap = lax.broadcasted_iota(jnp.int32, s2.shape, 0) - lax.broadcasted_iota(jnp.int32, s2.shape, 1)
                    prob = jnp.where(gap <= -shift, prob, 0.0)
                d_prob = dot_nt(v_own, do_blk)
                d_score = (prob * (d_prob - stat_ref[0, heads + h:heads + h + 1, pl.ds(base, blk)]) * scale).astype(BF)
                dv_h = dot_nn(prob.astype(BF), do_blk)
                dk_h = dot_nn(d_score, q_blk)
                dk_new = dk_h if dk_new is None else dk_new + dk_h
                dv_new = dv_h if dv_new is None else dv_new + dv_h
            return dk_new, dv_new

        dk_ref[...], dv_ref[...] = block(first, True)

        def step(j, carry):
            dk_new, dv_new = block(j, False)
            dk_ref[...] += dk_new
            dv_ref[...] += dv_new
            return carry

        lax.fori_loop(first + 1, n_blk, step, 0)
        d_raw, d_gain = head_norm_back(dk_ref[...], kraw_ref[0, rows, :], gain_ref[...], cos_ref[rows, :], sin_ref[rows, :])
        dkv_ref[0, rows, :hd] = d_raw
        dkv_ref[0, rows, hd:] = dv_ref[...].astype(BF)
        total = total + d_gain

    @pl.when(b == 0)
    def _():
        dgain_ref[...] = total

    @pl.when(b > 0)
    def _():
        dgain_ref[...] += total


def dkv_call(c_arr, kv_loc, stats, k_raw, k_norm, cos_t, sin_t, q_all, do_all, hd):
    nb, s, dkv = kv_loc.shape
    owners = q_all.shape[0]
    piece = s // 2
    row = lambda width: pl.BlockSpec((1, s, width), lambda b: (b, 0, 0))
    return pl.pallas_call(
        functools.partial(dkv_body, nb, owners, hd),
        grid=(nb,),
        in_specs=[pl.BlockSpec(memory_space=pltpu.SMEM), row(dkv), pl.BlockSpec((1,) + stats.shape[1:], lambda b: (b, 0, 0)), row(hd), const_spec(k_norm.shape), const_spec(cos_t.shape), const_spec(sin_t.shape), pl.BlockSpec(memory_space=pl.ANY), pl.BlockSpec(memory_space=pl.ANY)],
        out_specs=[row(dkv), pl.BlockSpec((1, hd), lambda b: (0, 0))],
        out_shape=[jax.ShapeDtypeStruct((nb, s, dkv), BF), jax.ShapeDtypeStruct((1, hd), F32)],
        scratch_shapes=[pltpu.VMEM((2, owners * s, q_all.shape[3]), BF), pltpu.VMEM((2, owners * s, q_all.shape[3]), BF), pltpu.SemaphoreType.DMA((2,)), pltpu.SemaphoreType.DMA((2,)), pltpu.VMEM((piece, hd), F32), pltpu.VMEM((piece, hd), F32)],
        compiler_params=params(),
        cost_estimate=pl.CostEstimate(flops=4 * nb * s * owners * s * q_all.shape[3], bytes_accessed=4 * q_all.size, transcendentals=nb * s * owners * s // 2),
        name="grad_kv",
    )(c_arr, kv_loc, stats, k_raw, k_norm, cos_t, sin_t, q_all, do_all)


def shift_by(arr, axis, n, amount):
    return lax.ppermute(arr, axis, [(i, (i + amount) % n) for i in range(n)])


def ring_gather(arr, axis, n):
    half = arr.shape[0] // 2
    prev = shift_by(arr, axis, n, 1)
    nxt = shift_by(arr, axis, n, -1)
    far_a = shift_by(prev[:half], axis, n, 1)
    far_b = shift_by(nxt[half:], axis, n, -1)
    return arr, prev, nxt, jnp.concatenate([far_a, far_b], axis=0)


def ring_ids(t, n):
    return [t, (t + n - 1) % n, (t + 1) % n, (t + 2) % n]


def place(blocks, ids, n):
    out = jnp.zeros((n,) + blocks[0].shape, blocks[0].dtype)
    for blk, i in zip(blocks, ids):
        out = lax.dynamic_update_slice(out, blk[None], (i,) + (0,) * blk.ndim)
    return out


def solution(mesh):
    n_dp, n_tp, n_cp = mesh.shape['dp'], mesh.shape['tp'], mesh.shape['cp']
    assert n_tp == 4 and n_cp % 2 == 0
    fine = Mesh(mesh.devices.reshape(n_dp, n_tp, n_cp // 2, 2), ('dp', 'tp', 'cx', 'cc'))
    CP = ('cx', 'cc')

    def per_device(hidden, cotangent, pos_loc, w_q, w_k, w_v, w_o, w_pre, w_post, q_norm, k_norm):
        hd = q_norm.shape[0]
        batch, s, d = hidden.shape
        dq, dk = w_q.shape[1], w_k.shape[1]
        t = lax.axis_index('tp')
        core = lax.axis_index('cc')
        c = lax.axis_index('cx') * 2 + core
        c_arr = jnp.full((1,), c, jnp.int32)
        ids = ring_ids(t, n_tp)
        t_arr = jnp.stack(ids).astype(jnp.int32)
        nc = 3 if batch % 3 == 0 else 1
        nb = batch // nc
        w_pre2, w_post2, qg2, kg2 = w_pre[None], w_post[None], q_norm[None], k_norm[None]

        half_dim = hd // 2
        inv_freq = 1.0 / (ROPE_SCALE * ROPE_BASE ** (jnp.arange(half_dim, dtype=F32) * (2.0 / hd)))
        angles = pos_loc.astype(F32)[:, None] * inv_freq[None, :]
        cos_t, sin_t = jnp.cos(angles), jnp.sin(angles)

        def gather_weight(half):
            blocks = ring_gather(half, 'tp', n_tp)
            mine = place(blocks, ids, n_tp)
            other = lax.ppermute(mine, 'cc', [(0, 1), (1, 0)])
            return jnp.where(core == 0, mine, other), jnp.where(core == 0, other, mine)

        wo_a, wo_b = gather_weight(lax.dynamic_slice(w_o, (core * (dq // 2), 0), (dq // 2, d)))
        w_full = jnp.concatenate([wo_a, wo_b], axis=1).reshape(n_tp * dq, d)

        pre, kv_all, att = [], [], []
        for i in range(nc):
            pre.append(pre_call(i * nb, nb, hidden, w_q, w_k, w_v, w_pre2, qg2, kg2, cos_t, sin_t))
            kv_all.append(lax.all_gather(pre[i][4], CP))
            att.append(fwd_call(c_arr, pre[i][3], kv_all[i], hd))
        o_blocks = [ring_gather(att[i][0], 'tp', n_tp) for i in range(nc)]

        q_all = []
        for i in range(nc):
            q_all.append(lax.all_gather(pre[i][3], CP))

        carried, d_outs, deltas, d_posts = None, [], [], []
        for i in range(nc):
            y, d_attn, d_out, delta, d_post = mid_call(i * nb, nb, hd, t_arr, o_blocks[i], att[i][1], hidden, cotangent, w_full, w_o, w_post2, carried)
            carried = (y, d_attn)
            d_outs.append(d_out)
            deltas.append(delta)
            d_posts.append(d_post)
        output, d_attn = carried
        d_post = sum(d_posts)

        do_all = []
        for i in range(nc):
            do_all.append(lax.all_gather(d_outs[i], CP))
        heads = dq // hd

        st = jnp.concatenate([jnp.concatenate([att[i][2], deltas[i]], axis=-1) for i in range(nc)], axis=0)
        st = jnp.tile(jnp.moveaxis(st, 2, 1), (1, 4, 1))
        st = lax.all_gather(st, CP)[:, :, :2 * heads]
        st = jnp.concatenate([st[..., :s // 2], st[..., s // 2:][::-1]], axis=0)
        stats = jnp.moveaxis(st, 0, 2).reshape(batch, 2 * heads, n_cp * s)

        w_qkv_t = jnp.concatenate([w_q, w_k, w_v], axis=1).T
        half_w = lax.dynamic_slice(w_qkv_t, (core * ((dq + 2 * dk) // 2), 0), ((dq + 2 * dk) // 2, d))
        half_w = lax.optimization_barrier((half_w, o_blocks[nc - 1][3]))[0]
        wt_q, wt_kv = gather_weight(half_w)
        wt_q, wt_kv = wt_q.reshape(n_tp * dq, d), wt_kv.reshape(n_tp * 2 * dk, d)

        o_full = jnp.concatenate([att[i][0] for i in range(nc)], axis=0).reshape(batch * s, dq)
        dw_o = lax.dot_general(o_full, d_attn.reshape(batch * s, d), (((0,), (0,)), ((), ())), preferred_element_type=F32)
        dw_o = lax.psum(dw_o, CP)

        gq = []
        for i in range(nc):
            gq.append(dq_call(c_arr, pre[i][3], d_outs[i], att[i][2], deltas[i], pre[i][1], qg2, cos_t, sin_t, kv_all[i], hd))
        gkv = []
        for i in range(nc):
            gkv.append(dkv_call(c_arr, pre[i][4], stats[i * nb:(i + 1) * nb], pre[i][2], kg2, cos_t, sin_t, q_all[i], do_all[i], hd))

        normed = jnp.concatenate([pre[i][0] for i in range(nc)], axis=0).reshape(batch * s, d)
        dq_flat = jnp.concatenate([g[0] for g in gq], axis=0).reshape(batch * s, dq)
        dkv_flat = jnp.concatenate([g[0] for g in gkv], axis=0).reshape(batch * s, 2 * dk)

        def weight_grad(cot):
            return lax.dot_general(normed, cot, (((0,), (0,)), ((), ())), preferred_element_type=F32)

        dq_flat, dkv_flat, dw_o = lax.optimization_barrier((dq_flat, dkv_flat, dw_o))
        dws = (weight_grad(dq_flat), weight_grad(dkv_flat[:, :dk]), weight_grad(dkv_flat[:, dk:]))
        dw_q, dw_k, dw_v = lax.psum(dws, CP)

        rows = nb * s
        quarter = rows // n_tp
        d_hidden = jnp.zeros((batch * s, d), BF)
        x_flat, gy_flat = hidden.reshape(batch * s, d), cotangent.reshape(batch * s, d)
        d_pre = jnp.zeros((d,), F32)

        def exchange(chunk):
            blocks = chunk.reshape(n_tp, quarter, chunk.shape[-1])
            take = lambda i: lax.dynamic_index_in_dim(blocks, i, 0, keepdims=False)
            recv = [take(t)]
            for amount in (1, n_tp - 1, 2):
                recv.append(shift_by(take((t + amount) % n_tp), 'tp', n_tp, amount))
            out = place(recv, [t, (t + n_tp - 1) % n_tp, (t + 1) % n_tp, (t + 2) % n_tp], n_tp)
            return jnp.moveaxis(out, 0, 1).reshape(quarter, n_tp * chunk.shape[-1])

        for i in range(nc):
            ex_q = exchange(gq[i][0].reshape(rows, dq))
            ex_kv = exchange(gkv[i][0].reshape(rows, 2 * dk))
            d_normed = dot_nn(ex_q, wt_q) + dot_nn(ex_kv, wt_kv)
            base = i * rows + t * quarter
            x = lax.dynamic_slice(x_flat, (base, 0), (quarter, d)).astype(F32)
            gy = lax.dynamic_slice(gy_flat, (base, 0), (quarter, d)).astype(F32)
            inv = rms_inv(x)
            unit = x * inv
            d_pre = d_pre + jnp.sum(d_normed * unit, axis=0)
            d_unit = d_normed * (1.0 + w_pre)
            dx = (gy + inv * (d_unit - unit * jnp.mean(d_unit * unit, axis=-1, keepdims=True))).astype(BF)
            for blk, j in zip(ring_gather(dx, 'tp', n_tp), ids):
                d_hidden = lax.dynamic_update_slice(d_hidden, blk, (i * rows + j * quarter, 0))

        small = jnp.concatenate([d_pre, sum(g[1] for g in gq)[0], sum(g[1] for g in gkv)[0]])
        for bit in (1, 2):
            small = small + lax.ppermute(small, 'tp', [(i, i ^ bit) for i in range(n_tp)])
        small, d_post = lax.psum((small, d_post), CP)
        d_pre, d_qnorm, d_knorm = small[:d], small[d:d + hd], small[d + hd:]
        return output, d_hidden.reshape(batch, s, d), dw_q, dw_k, dw_v, dw_o, d_pre, d_post[0], d_qnorm, d_knorm

    cp = ('cx', 'cc')
    specs_in = (P('dp', cp, None), P('dp', cp, None), P(('dp',) + cp), P(None, 'tp'), P(None, 'tp'), P(None, 'tp'), P('tp', None), P(None), P(None), P(None), P(None))
    specs_out = (P('dp', cp, None), P('dp', cp, None), P('dp', 'tp'), P('dp', 'tp'), P('dp', 'tp'), P(('dp', 'tp'), None), P('dp'), P('dp'), P('dp'), P('dp'))

    return jax.shard_map(per_device, mesh=fine, in_specs=specs_in, out_specs=specs_out, check_vma=False)
```

time: 2030 us -> 878 us (0.43)
  waiting for transfers between devices: 1250 us -> 281 us
  matrix products: 310 us -> 48.7 us
  Pallas kernels: 0 us -> 246 us
  other arithmetic: 134 us -> 59.3 us
  local copies, waits for them, and re-layouts: 168 us -> 105 us
  blocking collectives: 78.2 us -> 41.6 us
    psum x3 -> x2, waiting for transfers between devices: 738 us -> 71.7 us  [the longest x1 51.5 us: per_device(): dw_o = lax.psum(dw_o, CP)]
    ppermute x58 -> x54, waiting for transfers between devices: 507 us -> 136 us  [the longest x50 122 us: shift_by(): return lax.ppermute(arr, axis, [(i, (i + amount) % n) for i in range(n)])]
    dot_general x67 -> x10, matrix products: 310 us -> 48.7 us  [the longest x3 19.4 us: weight_grad(): lax.dot_general(normed, cot, (((0,), (0,)), ((), ())), preferred_element_...]
    pallas_call x0 -> x15, Pallas kernels: none -> 246 us  [the longest x3 73 us: mid_call(): pl.pallas_call(functools.partial(mid_body, hd), grid=(nb, 2), in_specs=in...]
    while x252 -> x0, local copies, waits for them, and re-layouts: 103 us -> none
    all_gather x0 -> x10, waiting for transfers between devices: none -> 69 us  [the longest x3 39.8 us: per_device(): do_all.append(lax.all_gather(d_outs[i], CP))]
    reduce_sum x16 -> x1, other arithmetic: 64 us -> 2.4 us  [rms_inv(): return lax.rsqrt(jnp.mean(values * values, axis=-1, keepdims=True) + EPS)]
    convert_element_type x4 -> x1, other arithmetic: 40.1 us -> 0.69 us  [per_device(): angles = pos_loc.astype(F32)[:, None] * inv_freq[None, :]]
  transfers between devices with their start and end apart: 61 -> 66, of which waited for: 31 -> 26; matrix products, arithmetic and copies ran while one was open for 15% -> 17% of each run, Pallas kernels for 0% -> 19%
where the time goes in v1:
time: 878 us; the launch traced here: 869 us
  waiting for transfers between devices  281 us (32%)
  Pallas kernels  246 us (28%)
  local copies, waits for them, and re-layouts  105 us (12%)
  starting transfers between devices  71.6 us (8%)
  other arithmetic  59.3 us (7%)
  matrix products  48.7 us (6%)
  blocking collectives  41.6 us (5%)
  between operations  15.7 us (2%)
    ppermute x50, waiting for transfers between devices, shift_by(): return lax.ppermute(arr, axis, [(i, (i + amount) % n) for i in range(n)])  122 us
    pallas_call x3, Pallas kernels, mid_call(): pl.pallas_call(functools.partial(mid_body, hd), grid=(nb, 2), in_specs=in...  73 us
    ppermute x50, starting transfers between devices, shift_by(): return lax.ppermute(arr, axis, [(i, (i + amount) % n) for i in range(n)])  63.5 us
    psum x1, waiting for transfers between devices, per_device(): dw_o = lax.psum(dw_o, CP)  51.5 us
    pallas_call x3, Pallas kernels, fwd_call(): pl.pallas_call(functools.partial(fwd_body, nb, owners, hd), grid=(nb,), i...  49.6 us
    pallas_call x3, Pallas kernels, dkv_call(): pl.pallas_call(functools.partial(dkv_body, nb, owners, hd), grid=(nb,), i...  47.8 us
    pallas_call x3, Pallas kernels, dq_call(): pl.pallas_call(functools.partial(dq_body, nb, owners, hd), grid=(nb,), in...  45.4 us
    psum x1, blocking collectives, per_device(): small, d_post = lax.psum((small, d_post), CP)  41.6 us
  transfers between devices with their start and end apart: 66, of which 26 were waited for; matrix products, arithmetic and copies ran while one was open for 17% of the time, Pallas kernels for 19%

profile of v1, /device:TPU:97, one launch (start us, length us, event | category | flops | bytes accessed | tf_op | source)
XLA Modules:
  0.0 869.4 jit_solution(8121005047911923934)
XLA Ops:
  10.8 9.7 %pre.3 = (bf16[2,384,2304]{2,1,0:T(8,128)(2,1)}, bf16[2,384,512]{2,1,0:T(8,128)(2,1)}, bf16[2,384,256]{2,1,0:T(8,128)(2,1)}, bf16[2,384,512]{2,1,0:T(8,128)(2,1)}, bf16[2,384,512]{2,1,0:T(8,128)(2,1)}) custom-call(bf16[6,384,2304]{2,1,0:T(8,128)(2,1)} %x_ref.11, bf16[2304,512]{1,0:T(8,128)(2,1)} %wq_ref.5, bf16[2304,256]{1,0:T(8,128)(2,1)} %wk_ref.5, ...), custom_call_target="tpu_custom_call" | custom-call | flops 3623878656 | bytes 7077888 | tf_op jit(solution)/shard_map/pre/pallas_call | solution.py:92
  20.6 9.8 %pre.5 = (bf16[2,384,2304]{2,1,0:T(8,128)(2,1)}, bf16[2,384,512]{2,1,0:T(8,128)(2,1)}, bf16[2,384,256]{2,1,0:T(8,128)(2,1)}, bf16[2,384,512]{2,1,0:T(8,128)(2,1)}, bf16[2,384,512]{2,1,0:T(8,128)(2,1)}) custom-call(bf16[6,384,2304]{2,1,0:T(8,128)(2,1)} %x_ref.11, bf16[2304,512]{1,0:T(8,128)(2,1)} %wq_ref.5, bf16[2304,256]{1,0:T(8,128)(2,1)} %wk_ref.5, ...), custom_call_target="tpu_custom_call" | custom-call | flops 3623878656 | bytes 7077888 | tf_op jit(solution)/shard_map/pre/pallas_call | solution.py:92
  30.6 10.5 %pre.4 = (bf16[2,384,2304]{2,1,0:T(8,128)(2,1)}, bf16[2,384,512]{2,1,0:T(8,128)(2,1)}, bf16[2,384,256]{2,1,0:T(8,128)(2,1)}, bf16[2,384,512]{2,1,0:T(8,128)(2,1)}, bf16[2,384,512]{2,1,0:T(8,128)(2,1)}) custom-call(bf16[6,384,2304]{2,1,0:T(8,128)(2,1)} %x_ref.11, bf16[2304,512]{1,0:T(8,128)(2,1)} %wq_ref.5, bf16[2304,256]{1,0:T(8,128)(2,1)} %wk_ref.5, ...), custom_call_target="tpu_custom_call" | custom-call | flops 3623878656 | bytes 7077888 | tf_op jit(solution)/shard_map/pre/pallas_call | solution.py:92
  49.9 25.8 %collective-permute-done.4 = bf16[256,2304]{1,0:T(8,128)(2,1)S(1)} collective-permute-done((bf16[256,2304]{1,0:T(8,128)(2,1)S(1)}, bf16[256,2304]{1,0:T(8,128)(2,1)S(1)}, u32[]{:S(2)}, u32[]{:S(2)}) %collective-permute-start.4) | collective-permute-done | bytes 1179680 | tf_op jit(solution)/shard_map/ppermute | solution.py:416
  81.0 9.9 %collective-permute-done.6 = bf16[128,2304]{1,0:T(8,128)(2,1)S(1)} collective-permute-done((bf16[128,2304]{1,0:T(8,128)(2,1)S(1)}, bf16[128,2304]{1,0:T(8,128)(2,1)S(1)}, u32[]{:S(2)}, u32[]{:S(2)}) %collective-permute-start.6) | collective-permute-done | bytes 589856 | tf_op jit(solution)/shard_map/ppermute | solution.py:416
  93.9 16.5 %attend.3 = (bf16[2,384,512]{2,1,0:T(8,128)(2,1)}, f32[2,384,512]{2,1,0:T(8,128)}, f32[2,384,2]{2,1,0:T(8,128)}) custom-call(s32[1]{0:T(128)} %bitcast.4.c_ref, bf16[2,384,512]{2,1,0:T(8,128)(2,1)} %get-tuple-element.65.q_ref, bf16[8,2,384,512]{3,2,1,0:T(8,128)(2,1)} %bitcast.228), custom_call_target="tpu_custom_call" | custom-call | flops 2415919104 | bytes 6291456 | tf_op jit(solution)/shard_map/attend/pallas_call | solution.py:192
  110.5 16.7 %attend.5 = (bf16[2,384,512]{2,1,0:T(8,128)(2,1)}, f32[2,384,512]{2,1,0:T(8,128)}, f32[2,384,2]{2,1,0:T(8,128)}) custom-call(s32[1]{0:T(128)} %bitcast.4.c_ref, bf16[2,384,512]{2,1,0:T(8,128)(2,1)} %get-tuple-element.73.q_ref, bf16[8,2,384,512]{3,2,1,0:T(8,128)(2,1)} %bitcast.226), custom_call_target="tpu_custom_call" | custom-call | flops 2415919104 | bytes 6291456 | tf_op jit(solution)/shard_map/attend/pallas_call | solution.py:192
  131.6 11.7 %all-gather.24.cloned.1.call-done = bf16[16,384,512]{2,1,0:T(8,128)(2,1)} async-done(((bf16[2,384,512]{2,1,0:T(8,128)(2,1)}), bf16[16,384,512]{2,1,0:T(8,128)(2,1)}) %all-gather.24.cloned.1.call-update) | async-done | bytes 6291472 | tf_op jit(solution)/shard_map/all_gather | solution.py:476
  143.3 16.4 %attend.4 = (bf16[2,384,512]{2,1,0:T(8,128)(2,1)}, f32[2,384,512]{2,1,0:T(8,128)}, f32[2,384,2]{2,1,0:T(8,128)}) custom-call(s32[1]{0:T(128)} %bitcast.4.c_ref, bf16[2,384,512]{2,1,0:T(8,128)(2,1)} %get-tuple-element.69.q_ref, bf16[8,2,384,512]{3,2,1,0:T(8,128)(2,1)} %bitcast.224), custom_call_target="tpu_custom_call" | custom-call | flops 2415919104 | bytes 6291456 | tf_op jit(solution)/shard_map/attend/pallas_call | solution.py:192
  165.6 4.4 broadcast_select_fusion.3
  173.6 6.6 collective-permute-done.9.o1_ref
  185.2 11.6 %collective-permute-done.1.o2_ref = bf16[2,384,512]{2,1,0:T(8,128)(2,1)} collective-permute-done((bf16[2,384,512]{2,1,0:T(8,128)(2,1)}, bf16[2,384,512]{2,1,0:T(8,128)(2,1)}, u32[]{:S(2)}, u32[]{:S(2)}) %collective-permute-start.1) | collective-permute-done | bytes 786464 | tf_op jit(solution)/shard_map/ppermute | solution.py:416
  201.9 3.9 pad_maximum_fusion.1
  215.7 6.3 collective-permute-done.3
  223.1 24.2 %mid.3 = (bf16[6,384,2304]{2,1,0:T(8,128)(2,1)}, bf16[6,384,2304]{2,1,0:T(8,128)(2,1)}, bf16[2,384,512]{2,1,0:T(8,128)(2,1)}, f32[2,384,2]{2,1,0:T(8,128)}, f32[1,2304]{1,0:T(1,128)}) custom-call(s32[4]{0:T(128)} %pad_add_fusion.t_ref, bf16[2,384,512]{2,1,0:T(8,128)(2,1)} %get-tuple-element.75.o0_ref, bf16[2,384,512]{2,1,0:T(8,128)(2,1)} %copy-done.20, ...), custom_call_target="tpu_custom_call" | custom-call | flops 9059696640 | bytes 17694720 | tf_op jit(solution)/shard_map/mid/pallas_call | solution.py:251
  247.3 24.3 %mid.4 = (bf16[6,384,2304]{2,1,0:T(8,128)(2,1)}, bf16[6,384,2304]{2,1,0:T(8,128)(2,1)}, bf16[2,384,512]{2,1,0:T(8,128)(2,1)}, f32[2,384,2]{2,1,0:T(8,128)}, f32[1,2304]{1,0:T(1,128)}) custom-call(s32[4]{0:T(128)} %pad_add_fusion.t_ref, bf16[2,384,512]{2,1,0:T(8,128)(2,1)} %get-tuple-element.71.o0_ref, ...), custom_call_target="tpu_custom_call", output_to_operand_aliasing={{0}: (11, {}), {1}: (12, {})} | custom-call | flops 9059696640 | bytes 17694720 | tf_op jit(solution)/shard_map/mid/pallas_call | solution.py:251
  271.7 24.5 %mid.5 = (bf16[6,384,2304]{2,1,0:T(8,128)(2,1)}, bf16[6,384,2304]{2,1,0:T(8,128)(2,1)}, bf16[2,384,512]{2,1,0:T(8,128)(2,1)}, f32[2,384,2]{2,1,0:T(8,128)}, f32[1,2304]{1,0:T(1,128)}) custom-call(s32[4]{0:T(128)} %pad_add_fusion.t_ref, bf16[2,384,512]{2,1,0:T(8,128)(2,1)} %get-tuple-element.67.o0_ref, ...), custom_call_target="tpu_custom_call", output_to_operand_aliasing={{0}: (11, {}), {1}: (12, {})} | custom-call | flops 9059696640 | bytes 17694720 | tf_op jit(solution)/shard_map/mid/pallas_call | solution.py:251
  313.1 9.4 %pad_maximum_fusion = bf16[6,384,2304]{2,1,0:T(8,128)(2,1)} fusion(bf16[2,384,2304]{2,1,0:T(8,128)(2,1)} %get-tuple-element.106, bf16[2,384,2304]{2,1,0:T(8,128)(2,1)} %get-tuple-element.105, bf16[2,384,2304]{2,1,0:T(8,128)(2,1)} %get-tuple-element.104), kind=kLoop, calls=%fused_computation | loop fusion | flops 10616832 | bytes 21233664 | tf_op jit(solution)/shard_map/concatenate | solution.py:522
  322.5 15.0 %grad_q.5 = (bf16[2,384,512]{2,1,0:T(8,128)(2,1)}, f32[1,256]{1,0:T(1,128)}) custom-call(s32[1]{0:T(128)} %bitcast.4.c_ref, bf16[2,384,512]{2,1,0:T(8,128)(2,1)} %get-tuple-element.65.q_ref, bf16[2,384,512]{2,1,0:T(8,128)(2,1)} %get-tuple-element.99.do_ref, f32[2,384,2]{2,1,0:T(8,128)} %get-tuple-element.90.lse_ref, ...), custom_call_target="tpu_custom_call" | custom-call | flops 3623878656 | bytes 6291456 | tf_op jit(solution)/shard_map/grad_q/pallas_call | solution.py:324
  345.3 15.2 %grad_q.3 = (bf16[2,384,512]{2,1,0:T(8,128)(2,1)}, f32[1,256]{1,0:T(1,128)}) custom-call(s32[1]{0:T(128)} %bitcast.4.c_ref, bf16[2,384,512]{2,1,0:T(8,128)(2,1)} %get-tuple-element.73.q_ref, bf16[2,384,512]{2,1,0:T(8,128)(2,1)} %get-tuple-element.82.do_ref, f32[2,384,2]{2,1,0:T(8,128)} %get-tuple-element.83.lse_ref, ...), custom_call_target="tpu_custom_call" | custom-call | flops 3623878656 | bytes 6291456 | tf_op jit(solution)/shard_map/grad_q/pallas_call | solution.py:324
  370.3 4.2 broadcast_in_dim.133
  378.9 4.3 copy.33
  387.4 8.6 collective-permute-done.22
  405.6 12.0 %convolution_bitcast_fusion = f32[512,2304]{1,0:T(8,128)} fusion(bf16[6,384,2304]{2,1,0:T(8,128)(2,1)} %get-tuple-element.107, bf16[2,384,512]{2,1,0:T(8,128)(2,1)} %get-tuple-element.67.o0_ref, bf16[2,384,512]{2,1,0:T(8,128)(2,1)S(1)} %copy-done.21, bf16[2,384,512]{2,1,0:T(8,128)(2,1)S(1)} %copy-done.26), kind=kOutput, calls=%fused_computation.4 | convolution fusion | flops 5438177280 | bytes 17694720 | tf_op jit(solution)/shard_map/dot_general | solution.py:512
  417.6 15.2 %grad_q.4 = (bf16[2,384,512]{2,1,0:T(8,128)(2,1)}, f32[1,256]{1,0:T(1,128)}) custom-call(s32[1]{0:T(128)} %bitcast.4.c_ref, bf16[2,384,512]{2,1,0:T(8,128)(2,1)} %get-tuple-element.69.q_ref, bf16[2,384,512]{2,1,0:T(8,128)(2,1)} %get-tuple-element.94.do_ref, f32[2,384,2]{2,1,0:T(8,128)} %get-tuple-element.88.lse_ref, ...), custom_call_target="tpu_custom_call" | custom-call | flops 3623878656 | bytes 6291456 | tf_op jit(solution)/shard_map/grad_q/pallas_call | solution.py:324
  451.4 5.2 collective-permute-done.32
  463.9 16.0 %grad_kv.5 = (bf16[2,384,512]{2,1,0:T(8,128)(2,1)}, f32[1,256]{1,0:T(1,128)}) custom-call(s32[1]{0:T(128)} %bitcast.4.c_ref, bf16[2,384,512]{2,1,0:T(8,128)(2,1)} %get-tuple-element.66.kv_ref, f32[2,4,3072]{2,1,0:T(4,128)} %slice.111.stat_ref, bf16[2,384,256]{2,1,0:T(8,128)(2,1)} %get-tuple-element.102.kraw_ref, f32[1,256]{1,0:T(1,128)} %bitcast.218, ...), custom_call_target="tpu_custom_call" | custom-call | flops 4831838208 | bytes 12582912 | tf_op jit(solution)/shard_map/grad_kv/pallas_call | solution.py:402
  484.2 15.9 %grad_kv.3 = (bf16[2,384,512]{2,1,0:T(8,128)(2,1)}, f32[1,256]{1,0:T(1,128)}) custom-call(s32[1]{0:T(128)} %bitcast.4.c_ref, bf16[2,384,512]{2,1,0:T(8,128)(2,1)} %get-tuple-element.74.kv_ref, f32[2,4,3072]{2,1,0:T(4,128)} %slice.103.stat_ref, bf16[2,384,256]{2,1,0:T(8,128)(2,1)} %get-tuple-element.92.kraw_ref, f32[1,256]{1,0:T(1,128)} %bitcast.219, ...), custom_call_target="tpu_custom_call" | custom-call | flops 4831838208 | bytes 12582912 | tf_op jit(solution)/shard_map/grad_kv/pallas_call | solution.py:402
  502.8 17.4 %all-gather.32.cloned.1.call-done = bf16[16,384,512]{2,1,0:T(8,128)(2,1)} async-done(((bf16[2,384,512]{2,1,0:T(8,128)(2,1)}), bf16[16,384,512]{2,1,0:T(8,128)(2,1)}) %all-gather.32.cloned.1.call-update) | async-done | bytes 6291472 | tf_op jit(solution)/shard_map/all_gather | solution.py:482
  520.3 39.8 %all-gather.34.cloned.1.call-done = bf16[16,384,512]{2,1,0:T(8,128)(2,1)} async-done(((bf16[2,384,512]{2,1,0:T(8,128)(2,1)}), bf16[16,384,512]{2,1,0:T(8,128)(2,1)}) %all-gather.34.cloned.1.call-update) | async-done | bytes 6291472 | tf_op jit(solution)/shard_map/all_gather | solution.py:496
  560.1 15.9 %grad_kv.4 = (bf16[2,384,512]{2,1,0:T(8,128)(2,1)}, f32[1,256]{1,0:T(1,128)}) custom-call(s32[1]{0:T(128)} %bitcast.4.c_ref, bf16[2,384,512]{2,1,0:T(8,128)(2,1)} %get-tuple-element.70.kv_ref, f32[2,4,3072]{2,1,0:T(4,128)} %slice.107.stat_ref, bf16[2,384,256]{2,1,0:T(8,128)(2,1)} %get-tuple-element.97.kraw_ref, f32[1,256]{1,0:T(1,128)} %bitcast.220, ...), custom_call_target="tpu_custom_call" | custom-call | flops 4831838208 | bytes 12582912 | tf_op jit(solution)/shard_map/grad_kv/pallas_call | solution.py:402
  578.8 51.5 %all-reduce.5.cloned.1.call-done = f32[512,2304]{1,0:T(8,128)} async-done(((f32[512,2304]{1,0:T(8,128)}), f32[512,2304]{1,0:T(8,128)}) %all-reduce.5.cloned.1.call-update) | async-done | bytes 4718608 | tf_op jit(solution)/shard_map/psum | solution.py:513
  630.3 10.6 %fusion.59 = f32[2304,512]{1,0:T(8,128)} fusion(bf16[2304,2304]{1,0:T(8,128)(2,1)} %bitcast.193, bf16[2304,512]{1,0:T(8,128)(2,1)} %bitcast.208), kind=kOutput, calls=%fused_computation.166 | convolution fusion | flops 5435817984 | bytes 17694720 | tf_op jit(solution)/shard_map/dot_general | solution.py:527
  652.4 3.6 collective-permute-done.35
  659.5 7.7 broadcast_select_fusion.1
  678.6 6.0 fusion.39
  684.6 4.8 broadcast_in_dim.129
  695.5 4.4 fusion.42
  699.8 12.4 %collective-permute-done.28 = bf16[192,2304]{1,0:T(8,128)(2,1)S(1)} collective-permute-done((bf16[192,2304]{1,0:T(8,128)(2,1)S(1)}, bf16[192,2304]{1,0:T(8,128)(2,1)S(1)}, u32[]{:S(2)}, u32[]{:S(2)}) %collective-permute-start.28) | collective-permute-done | bytes 884768 | tf_op jit(solution)/shard_map/ppermute | solution.py:416
  717.1 4.7 collective-permute-done.30
  728.3 4.4 fusion.44
  733.4 10.2 %collective-permute-done.38 = bf16[192,2304]{1,0:T(8,128)(2,1)S(1)} collective-permute-done((bf16[192,2304]{1,0:T(8,128)(2,1)S(1)}, bf16[192,2304]{1,0:T(8,128)(2,1)S(1)}, u32[]{:S(2)}, u32[]{:S(2)}) %collective-permute-start.38) | collective-permute-done | bytes 884768 | tf_op jit(solution)/shard_map/ppermute | solution.py:416
  748.5 4.8 collective-permute-done.40
  760.3 12.7 %collective-permute-done.52 = f32[2816]{0:T(1024)S(1)} collective-permute-done((f32[2816]{0:T(1024)S(1)}, f32[2816]{0:T(1024)S(1)}, u32[]{:S(2)}, u32[]{:S(2)}) %collective-permute-start.52) | collective-permute-done | bytes 11296 | tf_op jit(solution)/shard_map/ppermute | solution.py:565
  777.4 41.6 %all-reduce = (f32[2816]{0:T(1024)S(1)}, f32[2304]{0:T(1024)}) all-reduce(f32[2816]{0:T(1024)S(1)} %add.388, f32[2304]{0:T(1024)S(1)} %add_reduce_fusion), channel_id=1, replica_groups=mesh['dp'=1,'tp'=4,'cx'=4,'cc'=2] {'cx','cc'}, use_global_device_ids=true, to_apply=%region_13.14 | all-reduce | flops 5120 | bytes 40960 | tf_op jit(solution)/shard_map/psum | solution.py:566
  824.5 4.8 collective-permute-done.50
  830.6 20.2 %all-reduce.7.cloned.1.call-done = (f32[2304,512]{1,0:T(8,128)}, f32[2304,256]{1,0:T(8,128)}, f32[2304,256]{1,0:T(8,128)}) async-done(((f32[2304,512]{1,0:T(8,128)}, f32[2304,256]{1,0:T(8,128)}, f32[2304,256]{1,0:T(8,128)}), (f32[2304,512]{1,0:T(8,128)}, f32[2304,256]{1,0:T(8,128)}, f32[2304,256]{1,0:T(8,128)})) %all-reduce.7.cloned.1.call-update) | async-done | bytes 9437200 | tf_op jit(solution)/shard_map/psum | solution.py:531
  850.8 5.2 copy.99
  (366 shorter events, 217.0 us)
Async XLA Ops:
  7.2 86.7 %all-gather.22.cloned.1.call-start = ((), (), s32[]{:S(2)}) async-start(), calls=%async_computation.2 | async-start | bytes 7077888 | tf_op jit(solution)/shard_map/all_gather | solution.py:476
  20.6 89.9 %all-gather.26.cloned.1.call-start = ((), (), s32[]{:S(2)}) async-start(), calls=%async_computation.4 | async-start | bytes 7077888 | tf_op jit(solution)/shard_map/all_gather | solution.py:476
  30.5 112.8 %all-gather.24.cloned.1.call-start = ((), (), s32[]{:S(2)}) async-start(), calls=%async_computation.3 | async-start | bytes 7077888 | tf_op jit(solution)/shard_map/all_gather | solution.py:476
  41.2 418.9 %all-gather.20.cloned.1.call-start = ((), (), s32[]{:S(2)}) async-start(), calls=%async_computation | async-start | bytes 1327104 | tf_op jit(solution)/shard_map/all_gather | solution.py:501
  45.3 30.4 %collective-permute-start.4 = (bf16[256,2304]{1,0:T(8,128)(2,1)S(1)}, bf16[256,2304]{1,0:T(8,128)(2,1)S(1)}, u32[]{:S(2)}, u32[]{:S(2)}) collective-permute-start(bf16[256,2304]{1,0:T(8,128)(2,1)S(1)} %get-tuple-element.145), channel_id=1, source_target_pairs={{0,8},{8,16},{16,24},{24,0},{1,9},{9,17},{17,25},{25,1},{2,10},{10... | collective-permute-start | bytes 3538952 | tf_op jit(solution)/shard_map/ppermute | solution.py:416
  47.9 28.0 %collective-permute-start.5 = (bf16[256,2304]{1,0:T(8,128)(2,1)S(1)}, bf16[256,2304]{1,0:T(8,128)(2,1)S(1)}, u32[]{:S(2)}, u32[]{:S(2)}) collective-permute-start(bf16[256,2304]{1,0:T(8,128)(2,1)S(1)} %get-tuple-element.145), channel_id=1, source_target_pairs={{0,24},{8,0},{16,8},{24,16},{1,25},{9,1},{17,9},{25,17},{2,26},{10... | collective-permute-start | bytes 3538952 | tf_op jit(solution)/shard_map/ppermute | solution.py:416
  75.7 15.2 %collective-permute-start.6 = (bf16[128,2304]{1,0:T(8,128)(2,1)S(1)}, bf16[128,2304]{1,0:T(8,128)(2,1)S(1)}, u32[]{:S(2)}, u32[]{:S(2)}) collective-permute-start(bf16[128,2304]{1,0:T(8,128)(2,1)S(1)} %slice.121), channel_id=1, source_target_pairs={{0,8},{8,16},{16,24},{24,0},{1,9},{9,17},{17,25},{25,1},{2,10},{10... | collective-permute-start | bytes 1769480 | tf_op jit(solution)/shard_map/ppermute | solution.py:416
  75.9 15.0 %collective-permute-start.7 = (bf16[128,2304]{1,0:T(8,128)(2,1)S(1)}, bf16[128,2304]{1,0:T(8,128)(2,1)S(1)}, u32[]{:S(2)}, u32[]{:S(2)}) collective-permute-start(bf16[128,2304]{1,0:T(8,128)(2,1)S(1)} %slice.122), channel_id=1, source_target_pairs={{0,24},{8,0},{16,8},{24,16},{1,25},{9,1},{17,9},{25,17},{2,26},{10... | collective-permute-start | bytes 1769480 | tf_op jit(solution)/shard_map/ppermute | solution.py:416
  92.0 71.3 %collective-permute-start.8 = (bf16[4,256,2304]{2,1,0:T(8,128)(2,1)}, bf16[4,256,2304]{2,1,0:T(8,128)(2,1)}, u32[]{:S(2)}, u32[]{:S(2)}) collective-permute-start(bf16[4,256,2304]{2,1,0:T(8,128)(2,1)} %fusion.41), channel_id=1, source_target_pairs={{0,1},{1,0},{2,3},{3,2},{4,5},{5,4},{6,7},{7,6},{8,9},{9,8},{10,11... | collective-permute-start | bytes 14155784 | tf_op jit(solution)/shard_map/ppermute | solution.py:467
  110.4 50.7 %collective-permute-start = (bf16[2,384,512]{2,1,0:T(8,128)(2,1)}, bf16[2,384,512]{2,1,0:T(8,128)(2,1)S(1)}, u32[]{:S(2)}, u32[]{:S(2)}) collective-permute-start(bf16[2,384,512]{2,1,0:T(8,128)(2,1)} %get-tuple-element.67.o0_ref), channel_id=1, source_target_pairs={{0,8},{8,16},{16,24},{24,0},{1,9},{9,17},{17,25},{25,1},{2,10},{10... | collective-permute-start | bytes 2359304 | tf_op jit(solution)/shard_map/ppermute | solution.py:416
  127.3 37.3 %collective-permute-start.13 = (bf16[2,384,512]{2,1,0:T(8,128)(2,1)}, bf16[2,384,512]{2,1,0:T(8,128)(2,1)S(1)}, u32[]{:S(2)}, u32[]{:S(2)}) collective-permute-start(bf16[2,384,512]{2,1,0:T(8,128)(2,1)} %get-tuple-element.75.o0_ref), channel_id=1, source_target_pairs={{0,8},{8,16},{16,24},{24,0},{1,9},{9,17},{17,25},{25,1},{2,10},{10... | collective-permute-start | bytes 2359304 | tf_op jit(solution)/shard_map/ppermute | solution.py:416
  129.7 42.1 %collective-permute-start.14 = (bf16[2,384,512]{2,1,0:T(8,128)(2,1)}, bf16[2,384,512]{2,1,0:T(8,128)(2,1)}, u32[]{:S(2)}, u32[]{:S(2)}) collective-permute-start(bf16[2,384,512]{2,1,0:T(8,128)(2,1)} %get-tuple-element.75.o0_ref), channel_id=1, source_target_pairs={{0,24},{8,0},{16,8},{24,16},{1,25},{9,1},{17,9},{25,17},{2,26},{10... | collective-permute-start | bytes 2359304 | tf_op jit(solution)/shard_map/ppermute | solution.py:416
  159.7 20.4 %collective-permute-start.9 = (bf16[2,384,512]{2,1,0:T(8,128)(2,1)}, bf16[2,384,512]{2,1,0:T(8,128)(2,1)}, u32[]{:S(2)}, u32[]{:S(2)}) collective-permute-start(bf16[2,384,512]{2,1,0:T(8,128)(2,1)} %get-tuple-element.71.o0_ref), channel_id=1, source_target_pairs={{0,8},{8,16},{16,24},{24,0},{1,9},{9,17},{17,25},{25,1},{2,10},{10... | collective-permute-start | bytes 2359304 | tf_op jit(solution)/shard_map/ppermute | solution.py:416
  161.0 22.2 %collective-permute-start.10 = (bf16[2,384,512]{2,1,0:T(8,128)(2,1)}, bf16[2,384,512]{2,1,0:T(8,128)(2,1)}, u32[]{:S(2)}, u32[]{:S(2)}) collective-permute-start(bf16[2,384,512]{2,1,0:T(8,128)(2,1)} %get-tuple-element.71.o0_ref), channel_id=1, source_target_pairs={{0,24},{8,0},{16,8},{24,16},{1,25},{9,1},{17,9},{25,17},{2,26},{10... | collective-permute-start | bytes 2359304 | tf_op jit(solution)/shard_map/ppermute | solution.py:416
  163.3 33.5 %collective-permute-start.1 = (bf16[2,384,512]{2,1,0:T(8,128)(2,1)}, bf16[2,384,512]{2,1,0:T(8,128)(2,1)}, u32[]{:S(2)}, u32[]{:S(2)}) collective-permute-start(bf16[2,384,512]{2,1,0:T(8,128)(2,1)} %get-tuple-element.67.o0_ref), channel_id=1, source_target_pairs={{0,24},{8,0},{16,8},{24,16},{1,25},{9,1},{17,9},{25,17},{2,26},{10... | collective-permute-start | bytes 2359304 | tf_op jit(solution)/shard_map/ppermute | solution.py:416
  165.4 35.7 %collective-permute-start.2 = (bf16[1,384,512]{2,1,0:T(8,128)(2,1)}, bf16[1,384,512]{2,1,0:T(8,128)(2,1)S(1)}, u32[]{:S(2)}, u32[]{:S(2)}) collective-permute-start(bf16[1,384,512]{2,1,0:T(8,128)(2,1)} %slice.119), channel_id=1, source_target_pairs={{0,8},{8,16},{16,24},{24,0},{1,9},{9,17},{17,25},{25,1},{2,10},{10... | collective-permute-start | bytes 1179656 | tf_op jit(solution)/shard_map/ppermute | solution.py:416
  171.8 37.5 %collective-permute-start.15 = (bf16[1,384,512]{2,1,0:T(8,128)(2,1)}, bf16[1,384,512]{2,1,0:T(8,128)(2,1)}, u32[]{:S(2)}, u32[]{:S(2)}) collective-permute-start(bf16[1,384,512]{2,1,0:T(8,128)(2,1)} %slice.125), channel_id=1, source_target_pairs={{0,8},{8,16},{16,24},{24,0},{1,9},{9,17},{17,25},{25,1},{2,10},{10... | collective-permute-start | bytes 1179656 | tf_op jit(solution)/shard_map/ppermute | solution.py:416
  180.2 29.2 %collective-permute-start.16 = (bf16[1,384,512]{2,1,0:T(8,128)(2,1)}, bf16[1,384,512]{2,1,0:T(8,128)(2,1)}, u32[]{:S(2)}, u32[]{:S(2)}) collective-permute-start(bf16[1,384,512]{2,1,0:T(8,128)(2,1)} %slice.126), channel_id=1, source_target_pairs={{0,24},{8,0},{16,8},{24,16},{1,25},{9,1},{17,9},{25,17},{2,26},{10... | collective-permute-start | bytes 1179656 | tf_op jit(solution)/shard_map/ppermute | solution.py:416
  183.2 28.2 %collective-permute-start.11 = (bf16[1,384,512]{2,1,0:T(8,128)(2,1)}, bf16[1,384,512]{2,1,0:T(8,128)(2,1)}, u32[]{:S(2)}, u32[]{:S(2)}) collective-permute-start(bf16[1,384,512]{2,1,0:T(8,128)(2,1)} %slice.123), channel_id=1, source_target_pairs={{0,8},{8,16},{16,24},{24,0},{1,9},{9,17},{17,25},{25,1},{2,10},{10... | collective-permute-start | bytes 1179656 | tf_op jit(solution)/shard_map/ppermute | solution.py:416
  196.8 16.9 %collective-permute-start.12 = (bf16[1,384,512]{2,1,0:T(8,128)(2,1)}, bf16[1,384,512]{2,1,0:T(8,128)(2,1)}, u32[]{:S(2)}, u32[]{:S(2)}) collective-permute-start(bf16[1,384,512]{2,1,0:T(8,128)(2,1)} %slice.124), channel_id=1, source_target_pairs={{0,24},{8,0},{16,8},{24,16},{1,25},{9,1},{17,9},{25,17},{2,26},{10... | collective-permute-start | bytes 1179656 | tf_op jit(solution)/shard_map/ppermute | solution.py:416
  201.2 20.9 %collective-permute-start.3 = (bf16[1,384,512]{2,1,0:T(8,128)(2,1)}, bf16[1,384,512]{2,1,0:T(8,128)(2,1)}, u32[]{:S(2)}, u32[]{:S(2)}) collective-permute-start(bf16[1,384,512]{2,1,0:T(8,128)(2,1)} %slice.120), channel_id=1, source_target_pairs={{0,24},{8,0},{16,8},{24,16},{1,25},{9,1},{17,9},{25,17},{2,26},{10... | collective-permute-start | bytes 1179656 | tf_op jit(solution)/shard_map/ppermute | solution.py:416
  298.4 165.5 %all-gather.36.cloned.1.call-start = ((), (), s32[]{:S(2)}) async-start(), calls=%async_computation.9 | async-start | bytes 7077888 | tf_op jit(solution)/shard_map/all_gather | solution.py:482
  299.1 164.9 %all-gather.38.cloned.1.call-start = ((), (), s32[]{:S(2)}) async-start(), calls=%async_computation.10 | async-start | bytes 7077888 | tf_op jit(solution)/shard_map/all_gather | solution.py:496
  299.7 184.5 %all-gather.28.cloned.1.call-start = ((), (), s32[]{:S(2)}) async-start(), calls=%async_computation.5 | async-start | bytes 7077888 | tf_op jit(solution)/shard_map/all_gather | solution.py:482
  300.5 183.7 %all-gather.30.cloned.1.call-start = ((), (), s32[]{:S(2)}) async-start(), calls=%async_computation.6 | async-start | bytes 7077888 | tf_op jit(solution)/shard_map/all_gather | solution.py:496
  301.3 218.9 %all-gather.32.cloned.1.call-start = ((), (), s32[]{:S(2)}) async-start(), calls=%async_computation.7 | async-start | bytes 7077888 | tf_op jit(solution)/shard_map/all_gather | solution.py:482
  302.1 257.9 %all-gather.34.cloned.1.call-start = ((), (), s32[]{:S(2)}) async-start(), calls=%async_computation.8 | async-start | bytes 7077888 | tf_op jit(solution)/shard_map/all_gather | solution.py:496
  302.8 327.5 %all-reduce.5.cloned.1.call-start = ((), (), s32[]{:S(2)}) async-start(), calls=%async_computation.1 | async-start | bytes 9437184 | tf_op jit(solution)/shard_map/psum | solution.py:513
  308.7 53.9 %collective-permute-start.20 = (bf16[512,2304]{0,1:T(8,128)(2,1)}, bf16[512,2304]{0,1:T(8,128)(2,1)}, u32[]{:S(2)}, u32[]{:S(2)}) collective-permute-start(bf16[512,2304]{0,1:T(8,128)(2,1)} %fusion.5), channel_id=1, source_target_pairs={{0,8},{8,16},{16,24},{24,0},{1,9},{9,17},{17,25},{25,1},{2,10},{10... | collective-permute-start | bytes 7077896 | tf_op jit(solution)/shard_map/ppermute | solution.py:416
  310.0 55.6 %collective-permute-start.21 = (bf16[512,2304]{0,1:T(8,128)(2,1)}, bf16[512,2304]{0,1:T(8,128)(2,1)}, u32[]{:S(2)}, u32[]{:S(2)}) collective-permute-start(bf16[512,2304]{0,1:T(8,128)(2,1)} %fusion.5), channel_id=1, source_target_pairs={{0,24},{8,0},{16,8},{24,16},{1,25},{9,1},{17,9},{25,17},{2,26},{10... | collective-permute-start | bytes 7077896 | tf_op jit(solution)/shard_map/ppermute | solution.py:416
  339.7 99.5 %collective-permute-start.42 = (bf16[192,512]{1,0:T(8,128)(2,1)}, bf16[192,512]{1,0:T(8,128)(2,1)}, u32[]{:S(2)}, u32[]{:S(2)}) collective-permute-start(bf16[192,512]{1,0:T(8,128)(2,1)} %get-tuple-element.170), channel_id=1, source_target_pairs={{0,8},{8,16},{16,24},{24,0},{1,9},{9,17},{17,25},{25,1},{2,10},{10... | collective-permute-start | bytes 589832 | tf_op jit(solution)/shard_map/ppermute | solution.py:416
  339.7 103.4 %collective-permute-start.43 = (bf16[192,512]{1,0:T(8,128)(2,1)}, bf16[192,512]{1,0:T(8,128)(2,1)}, u32[]{:S(2)}, u32[]{:S(2)}) collective-permute-start(bf16[192,512]{1,0:T(8,128)(2,1)} %get-tuple-element.169), channel_id=1, source_target_pairs={{0,24},{8,0},{16,8},{24,16},{1,25},{9,1},{17,9},{25,17},{2,26},{10... | collective-permute-start | bytes 589832 | tf_op jit(solution)/shard_map/ppermute | solution.py:416
  342.4 102.4 %collective-permute-start.44 = (bf16[192,512]{1,0:T(8,128)(2,1)S(1)}, bf16[192,512]{1,0:T(8,128)(2,1)}, u32[]{:S(2)}, u32[]{:S(2)}) collective-permute-start(bf16[192,512]{1,0:T(8,128)(2,1)S(1)} %get-tuple-element.168), channel_id=1, source_target_pairs={{0,16},{8,24},{16,0},{24,8},{1,17},{9,25},{17,1},{25,9},{2,18},{10... | collective-permute-start | bytes 589832 | tf_op jit(solution)/shard_map/ppermute | solution.py:416
  365.0 31.0 %collective-permute-start.22 = (bf16[256,2304]{0,1:T(8,128)(2,1)}, bf16[256,2304]{0,1:T(8,128)(2,1)}, u32[]{:S(2)}, u32[]{:S(2)}) collective-permute-start(bf16[256,2304]{0,1:T(8,128)(2,1)} %slice.127), channel_id=1, source_target_pairs={{0,8},{8,16},{16,24},{24,0},{1,9},{9,17},{17,25},{25,1},{2,10},{10... | collective-permute-start | bytes 3538952 | tf_op jit(solution)/shard_map/ppermute | solution.py:416
  367.9 28.1 %collective-permute-start.23 = (bf16[256,2304]{0,1:T(8,128)(2,1)}, bf16[256,2304]{0,1:T(8,128)(2,1)}, u32[]{:S(2)}, u32[]{:S(2)}) collective-permute-start(bf16[256,2304]{0,1:T(8,128)(2,1)} %slice.128), channel_id=1, source_target_pairs={{0,24},{8,0},{16,8},{24,16},{1,25},{9,1},{17,9},{25,17},{2,26},{10... | collective-permute-start | bytes 3538952 | tf_op jit(solution)/shard_map/ppermute | solution.py:416
  396.0 49.9 %collective-permute-start.17 = (bf16[192,512]{1,0:T(8,128)(2,1)}, bf16[192,512]{1,0:T(8,128)(2,1)}, u32[]{:S(2)}, u32[]{:S(2)}) collective-permute-start(bf16[192,512]{1,0:T(8,128)(2,1)} %get-tuple-element.154), channel_id=1, source_target_pairs={{0,8},{8,16},{16,24},{24,0},{1,9},{9,17},{17,25},{25,1},{2,10},{10... | collective-permute-start | bytes 589832 | tf_op jit(solution)/shard_map/ppermute | solution.py:416
  403.6 255.9 %collective-permute-start.24 = (bf16[4,512,2304]{2,1,0:T(8,128)(2,1)}, bf16[4,512,2304]{2,1,0:T(8,128)(2,1)}, u32[]{:S(2)}, u32[]{:S(2)}) collective-permute-start(bf16[4,512,2304]{2,1,0:T(8,128)(2,1)} %constant_dynamic-update-slice_fusion.9), channel_id=1, source_target_pairs={{0,1},{1,0},{2,3},{3,2},{4,5},{5,4},{6,7},{7,6},{8,9},{9,8},{10,11... | collective-permute-start | bytes 28311560 | tf_op jit(solution)/shard_map/ppermute | solution.py:467
  436.0 414.9 %all-reduce.7.cloned.1.call-start = ((), (), s32[]{:S(2)}) async-start(), calls=%async_computation.11 | async-start | bytes 18874368 | tf_op jit(solution)/shard_map/psum | solution.py:531
  481.3 159.8 %collective-permute-start.45 = (bf16[192,512]{1,0:T(8,128)(2,1)S(1)}, bf16[192,512]{1,0:T(8,128)(2,1)}, u32[]{:S(2)}, u32[]{:S(2)}) collective-permute-start(bf16[192,512]{1,0:T(8,128)(2,1)S(1)} %get-tuple-element.174), channel_id=1, source_target_pairs={{0,8},{8,16},{16,24},{24,0},{1,9},{9,17},{17,25},{25,1},{2,10},{10... | collective-permute-start | bytes 589832 | tf_op jit(solution)/shard_map/ppermute | solution.py:416
  482.3 162.4 %collective-permute-start.46 = (bf16[192,512]{1,0:T(8,128)(2,1)S(1)}, bf16[192,512]{1,0:T(8,128)(2,1)}, u32[]{:S(2)}, u32[]{:S(2)}) collective-permute-start(bf16[192,512]{1,0:T(8,128)(2,1)S(1)} %get-tuple-element.173), channel_id=1, source_target_pairs={{0,24},{8,0},{16,8},{24,16},{1,25},{9,1},{17,9},{25,17},{2,26},{10... | collective-permute-start | bytes 589832 | tf_op jit(solution)/shard_map/ppermute | solution.py:416
  484.0 162.1 %collective-permute-start.47 = (bf16[192,512]{1,0:T(8,128)(2,1)S(1)}, bf16[192,512]{1,0:T(8,128)(2,1)}, u32[]{:S(2)}, u32[]{:S(2)}) collective-permute-start(bf16[192,512]{1,0:T(8,128)(2,1)S(1)} %get-tuple-element.172), channel_id=1, source_target_pairs={{0,16},{8,24},{16,0},{24,8},{1,17},{9,25},{17,1},{25,9},{2,18},{10... | collective-permute-start | bytes 589832 | tf_op jit(solution)/shard_map/ppermute | solution.py:416
  502.2 145.7 %collective-permute-start.25 = (bf16[192,512]{1,0:T(8,128)(2,1)}, bf16[192,512]{1,0:T(8,128)(2,1)}, u32[]{:S(2)}, u32[]{:S(2)}) collective-permute-start(bf16[192,512]{1,0:T(8,128)(2,1)} %get-tuple-element.158), channel_id=1, source_target_pairs={{0,8},{8,16},{16,24},{24,0},{1,9},{9,17},{17,25},{25,1},{2,10},{10... | collective-permute-start | bytes 589832 | tf_op jit(solution)/shard_map/ppermute | solution.py:416
  692.5 19.7 %collective-permute-start.28 = (bf16[192,2304]{1,0:T(8,128)(2,1)S(1)}, bf16[192,2304]{1,0:T(8,128)(2,1)S(1)}, u32[]{:S(2)}, u32[]{:S(2)}) collective-permute-start(bf16[192,2304]{1,0:T(8,128)(2,1)S(1)} %get-tuple-element.143), channel_id=1, source_target_pairs={{0,8},{8,16},{16,24},{24,0},{1,9},{9,17},{17,25},{25,1},{2,10},{10... | collective-permute-start | bytes 2654216 | tf_op jit(solution)/shard_map/ppermute | solution.py:416
  693.1 19.3 %collective-permute-start.29 = (bf16[192,2304]{1,0:T(8,128)(2,1)S(1)}, bf16[192,2304]{1,0:T(8,128)(2,1)S(1)}, u32[]{:S(2)}, u32[]{:S(2)}) collective-permute-start(bf16[192,2304]{1,0:T(8,128)(2,1)S(1)} %get-tuple-element.143), channel_id=1, source_target_pairs={{0,24},{8,0},{16,8},{24,16},{1,25},{9,1},{17,9},{25,17},{2,26},{10... | collective-permute-start | bytes 2654216 | tf_op jit(solution)/shard_map/ppermute | solution.py:416
  725.6 18.0 %collective-permute-start.38 = (bf16[192,2304]{1,0:T(8,128)(2,1)S(1)}, bf16[192,2304]{1,0:T(8,128)(2,1)S(1)}, u32[]{:S(2)}, u32[]{:S(2)}) collective-permute-start(bf16[192,2304]{1,0:T(8,128)(2,1)S(1)} %get-tuple-element.141), channel_id=1, source_target_pairs={{0,8},{8,16},{16,24},{24,0},{1,9},{9,17},{17,25},{25,1},{2,10},{10... | collective-permute-start | bytes 2654216 | tf_op jit(solution)/shard_map/ppermute | solution.py:416
  725.6 18.2 %collective-permute-start.39 = (bf16[192,2304]{1,0:T(8,128)(2,1)S(1)}, bf16[192,2304]{1,0:T(8,128)(2,1)S(1)}, u32[]{:S(2)}, u32[]{:S(2)}) collective-permute-start(bf16[192,2304]{1,0:T(8,128)(2,1)S(1)} %get-tuple-element.141), channel_id=1, source_target_pairs={{0,24},{8,0},{16,8},{24,16},{1,25},{9,1},{17,9},{25,17},{2,26},{10... | collective-permute-start | bytes 2654216 | tf_op jit(solution)/shard_map/ppermute | solution.py:416
  757.4 62.2 %collective-permute-start.48 = (bf16[192,2304]{1,0:T(8,128)(2,1)S(1)}, bf16[192,2304]{1,0:T(8,128)(2,1)S(1)}, u32[]{:S(2)}, u32[]{:S(2)}) collective-permute-start(bf16[192,2304]{1,0:T(8,128)(2,1)S(1)} %get-tuple-element.139), channel_id=1, source_target_pairs={{0,8},{8,16},{16,24},{24,0},{1,9},{9,17},{17,25},{25,1},{2,10},{10... | collective-permute-start | bytes 2654216 | tf_op jit(solution)/shard_map/ppermute | solution.py:416
  758.1 61.7 %collective-permute-start.49 = (bf16[192,2304]{1,0:T(8,128)(2,1)S(1)}, bf16[192,2304]{1,0:T(8,128)(2,1)S(1)}, u32[]{:S(2)}, u32[]{:S(2)}) collective-permute-start(bf16[192,2304]{1,0:T(8,128)(2,1)S(1)} %get-tuple-element.139), channel_id=1, source_target_pairs={{0,24},{8,0},{16,8},{24,16},{1,25},{9,1},{17,9},{25,17},{2,26},{10... | collective-permute-start | bytes 2654216 | tf_op jit(solution)/shard_map/ppermute | solution.py:416
  (74 other events, 633.8 us)
Sparse Core Ops, SparseCore 0:
  20.7 42.6 all-gather.21
  64.9 38.3 all-gather.25
  104.9 38.3 all-gather.23
  298.6 21.9 all-gather.19
  322.0 38.3 all-gather.35
  361.9 38.4 all-gather.37
  401.9 38.3 all-gather.27
  441.9 38.3 all-gather.29
  481.9 38.3 all-gather.31
  521.7 38.3 all-gather.33
  563.1 67.2 all-reduce.4
  732.9 117.8 all-reduce.6
